TPU v7x, 16 devices: a 4x2x1 block of a 4x4x8 slice. The times are simulated.
16 devices in a mesh: rep: 4 (over y, z, core), dp: 4 (over x).
Axes of the slice: x: 4, y: 2, z: 1, core: 2. Of those that a mesh axis runs over, the one named last changes fastest.
The devices are a block of a 4x4x8 slice.
Arguments:
- x: bfloat16 [16, 4096, 1024], P(('rep', 'dp')), parts along dimension 0
- dy: bfloat16 [16, 4096, 1024], P(('rep', 'dp')), parts along dimension 0
- w_gate: bfloat16 [2, 1024, 3200], replicated
- w_up: bfloat16 [2, 1024, 3200], replicated
- w_down: bfloat16 [2, 3200, 1024], replicated
- m_w_gate: float32 [2, 1024, 3200], P(None, 'dp')
- m_w_up: float32 [2, 1024, 3200], P(None, 'dp')
- m_w_down: float32 [2, 3200, 1024], P(None, 'dp')
- v_w_gate: float32 [2, 1024, 3200], P(None, 'dp')
- v_w_up: float32 [2, 1024, 3200], P(None, 'dp')
- v_w_down: float32 [2, 3200, 1024], P(None, 'dp')
Outputs:
- output 1: bfloat16 [8, 1024, 3200], P('rep'), parts along dimension 0
- output 2: bfloat16 [8, 1024, 3200], P('rep'), parts along dimension 0
- output 3: bfloat16 [8, 3200, 1024], P('rep'), parts along dimension 0
- output 4: float32 [8, 1024, 3200], P('rep', 'dp'), parts along dimension 0
- output 5: float32 [8, 1024, 3200], P('rep', 'dp'), parts along dimension 0
- output 6: float32 [8, 3200, 1024], P('rep', 'dp'), parts along dimension 0
- output 7: float32 [8, 1024, 3200], P('rep', 'dp'), parts along dimension 0
- output 8: float32 [8, 1024, 3200], P('rep', 'dp'), parts along dimension 0
- output 9: float32 [8, 3200, 1024], P('rep', 'dp'), parts along dimension 0
There are 4 independent parts. A program takes and returns all parts, laid end to end along the dimension named above; an argument that names none is the same for every part.
All inputs are finite; a program needn't handle non-finite values.
Results may differ from a plain program's by a relative error of at most 0.022.
Values are sent between devices in bfloat16 or wider.
A program may use at most 768 MiB of HBM per device.

v0:
```python
import jax
import jax.numpy as jnp
from jax import lax

NAMES = ("w_gate", "w_up", "w_down")


def matmul(a, w):
    return jnp.dot(a, w, preferred_element_type=jnp.float32).astype(jnp.bfloat16)


def normed(h):
    wide = h.astype(jnp.float32)
    scale = lax.rsqrt(jnp.mean(wide**2, -1, keepdims=True) + 1e-6)
    return (wide * scale).astype(jnp.bfloat16)


def layer(h, w):
    a = normed(h)
    gate = jnp.dot(a, w["w_gate"], preferred_element_type=jnp.float32)
    up = jnp.dot(a, w["w_up"], preferred_element_type=jnp.float32)
    return h + matmul((jax.nn.silu(gate) * up).astype(jnp.bfloat16), w["w_down"])


def adamw(w, m, v, g):
    m = 0.9 * m + 0.1 * g
    v = 0.95 * v + 0.05 * g * g
    step = m * lax.rsqrt(v + 1e-8) + 0.1 * w
    return (w - 0.02 * step).astype(jnp.bfloat16), m, v


def clipped(gradients, sum_of_squares, count):
    factor = jnp.minimum(1.0, 0.5 * lax.rsqrt(sum_of_squares / count + 1e-30))
    return [g * factor for g in gradients]


def stack(weights, h):
    for number in range(weights["w_gate"].shape[0]):
        h = layer(h, {name: w[number] for name, w in weights.items()})
    return h


def solution(mesh):
    groups = mesh.shape["rep"]

    def step(x, dy, *arrays):
        weights, m, v = (arrays[i : i + 3] for i in (0, 3, 6))
        x, dy = (t.reshape(groups, -1, *t.shape[1:]) for t in (x, dy))

        def of_a_group(x, dy):
            _, back = jax.vjp(lambda w: stack(w, x), dict(zip(NAMES, weights, strict=True)))
            by_weights = back(dy)[0]
            gradients = [by_weights[name].astype(jnp.float32) for name in NAMES]
            gradients = clipped(gradients, sum(jnp.sum(g * g) for g in gradients), sum(g.size for g in gradients))
            new = [adamw(w.astype(jnp.float32), m, v, g) for w, m, v, g in zip(weights, m, v, gradients, strict=True)]
            return tuple(one[which] for which in range(3) for one in new)

        return tuple(t.reshape(-1, *t.shape[2:]) for t in jax.vmap(of_a_group)(x, dy))

    return step
```

profile of v0, /device:TPU:112, one launch (start us, length us, event | category | flops | bytes accessed | tf_op | source)
XLA Modules:
  0.0 1608.5 jit_solution(8549963528053595874)
XLA Ops:
  7.2 0.1 reduce-scatter.29.cloned.1.call-start
  7.3 5.1 fusion.35
  12.4 12.0 copy
  24.4 37.4 %fusion.104 = f32[4096,3200]{1,0:T(8,128)} fusion(bf16[2,1024,3200]{2,1,0:T(8,128)(2,1)} %param, bf16[1,4096,1024]{2,1,0:T(8,128)(2,1)} %param.2, f32[4096]{0:T(1024)S(1)} %add_rsqrt_fusion), kind=kOutput, calls=%fused_computation.129 | convolution fusion | flops 26856128512 | bytes 67387392 | tf_op jit(solution)/vmap(jvp())/dot_general | solution.py:20
  61.9 35.3 %fusion.102 = f32[4096,3200]{1,0:T(8,128)} fusion(bf16[2,1024,3200]{2,1,0:T(8,128)(2,1)S(1)} %bitcast.379, bf16[1,4096,1024]{2,1,0:T(8,128)(2,1)} %param.2, f32[4096]{0:T(1024)S(1)} %add_rsqrt_fusion), kind=kOutput, calls=%fused_computation.127 | convolution fusion | flops 26856128512 | bytes 67387392 | tf_op jit(solution)/vmap(jvp())/dot_general | solution.py:21
  97.1 42.2 %fusion.26 = bf16[4096,3200]{1,0:T(8,128)(2,1)} fusion(f32[4096,3200]{1,0:T(8,128)} %fusion.102, f32[4096,3200]{1,0:T(8,128)} %fusion.104), kind=kLoop, calls=%fused_computation.41 | loop fusion | flops 78643200 | bytes 131072000
  139.4 37.7 %fusion.39 = (f32[4096]{0:T(1024)S(1)}, bf16[1,1,4096,1024]{2,3,1,0:T(8,128)(2,1)}) fusion(bf16[4096,3200]{1,0:T(8,128)(2,1)} %fusion.26, bf16[2,3200,1024]{2,1,0:T(8,128)(2,1)} %param.4, bf16[1,4096,1024]{1,2,0:T(8,128)(2,1)} %copy), kind=kOutput, calls=%fused_computation.56 | convolution fusion | flops 26864513024 | bytes 49561600 | tf_op jit(solution)/vmap(jvp())/dot_general | solution.py:9
  177.1 0.6 copy-done.7
  177.7 37.8 %fusion.92 = f32[4096,3200]{1,0:T(8,128)} fusion(bf16[2,1024,3200]{2,1,0:T(8,128)(2,1)} %param, bf16[1,1,4096,1024]{2,3,1,0:T(8,128)(2,1)} %get-tuple-element.10, f32[4096]{0:T(1024)S(1)} %bitcast.385), kind=kOutput, calls=%fused_computation.117 | convolution fusion | flops 26856128512 | bytes 67387392 | tf_op jit(solution)/vmap(jvp())/dot_general | solution.py:20
  215.5 37.1 %fusion.96 = f32[4096,3200]{1,0:T(8,128)} fusion(bf16[2,1024,3200]{2,1,0:T(8,128)(2,1)} %param.3, bf16[1,1,4096,1024]{2,3,1,0:T(8,128)(2,1)S(1)} %copy-done.5, f32[4096]{0:T(1024)S(1)} %bitcast.386), kind=kOutput, calls=%fused_computation.121 | convolution fusion | flops 26856128512 | bytes 67387392 | tf_op jit(solution)/vmap(jvp())/dot_general | solution.py:21
  252.6 36.4 %convolution_convert_fusion.1 = bf16[4096,3200]{1,0:T(8,128)(2,1)} fusion(bf16[1,4096,1024]{2,1,0:T(8,128)(2,1)} %param.5, bf16[2,3200,1024]{2,1,0:T(8,128)(2,1)} %param.4), kind=kOutput, calls=%fused_computation.36 | convolution fusion | flops 26856652800 | bytes 41156608 | tf_op jit(solution)/vmap(transpose(jvp()))/dot_general | solution.py:9
  289.0 12.0 copy.1
  301.0 53.3 %fusion.6 = bf16[4096,3200]{1,0:T(8,128)(2,1)} fusion(f32[4096,3200]{1,0:T(8,128)} %fusion.92, f32[4096,3200]{1,0:T(8,128)} %fusion.96, bf16[4096,3200]{1,0:T(8,128)(2,1)} %convolution_convert_fusion.1), kind=kLoop, calls=%fused_computation.11 | loop fusion | flops 157286400 | bytes 157286400
  354.3 33.5 %fusion.94 = bf16[4096,1024]{0,1:T(8,128)(2,1)} fusion(bf16[4096,3200]{1,0:T(8,128)(2,1)} %fusion.6, bf16[2,1024,3200]{2,1,0:T(8,128)(2,1)S(1)} %bitcast.381), kind=kOutput, calls=%fused_computation.119 | convolution fusion | flops 26843545600 | bytes 41156608 | tf_op jit(solution)/vmap(transpose(jvp()))/dot_general | solution.py:20
  387.9 43.4 %fusion.41 = (f32[4096]{0:T(1024)S(1)}, bf16[4096,1024]{0,1:T(8,128)(2,1)}) fusion(bf16[1,1,4096,1024]{2,3,1,0:T(8,128)(2,1)} %get-tuple-element.10, bf16[4096,1024]{0,1:T(8,128)(2,1)} %fusion.94, bf16[2,1024,3200]{2,1,0:T(8,128)(2,1)} %param.3, bf16[4096,3200]{1,0:T(8,128)(2,1)} %convolution_convert_fusion.1, f32[4096,3200]{1,0:T(8,128)} %fusion.92), kind=kOutput, calls=%fused_computation.58 | convolution fusion | flops 26947350528 | bytes 110379008 | tf_op jit(solution)/vmap(transpose(jvp()))/dot_general | solution.py:21
  431.3 10.9 fusion.57
  442.3 3.4 copy-done.6
  445.6 32.3 %convolution_bitcast_fusion = f32[1,3200,1024]{2,1,0:T(8,128)} fusion(bf16[4096,3200]{1,0:T(8,128)(2,1)} %fusion.26, bf16[4096,1024]{0,1:T(8,128)(2,1)S(1)} %fusion.57), kind=kOutput, calls=%fused_computation.67 | convolution fusion | flops 26843545600 | bytes 47710208 | tf_op jit(solution)/vmap(transpose(jvp()))/dot_general | solution.py:9
  478.0 0.1 reduce-scatter.27.cloned.1.call-start
  478.1 46.1 %fusion.42 = f32[1,3200,1024]{2,1,0:T(8,128)} fusion(f32[4096,3200]{1,0:T(8,128)} %fusion.96, f32[4096,3200]{1,0:T(8,128)} %fusion.92, bf16[1,4096,1024]{2,1,0:T(8,128)(2,1)} %param.5), kind=kOutput, calls=%fused_computation.63 | convolution fusion | flops 26922188800 | bytes 126353408 | tf_op jit(solution)/vmap(transpose(jvp()))/dot_general | solution.py:9
  524.3 0.1 reduce-scatter.25.cloned.1.call-start
  524.3 35.6 %convolution_convert_fusion = bf16[4096,3200]{1,0:T(8,128)(2,1)} fusion(bf16[4096,1024]{0,1:T(8,128)(2,1)} %copy-done.6, bf16[2,3200,1024]{2,1,0:T(8,128)(2,1)} %param.4), kind=kOutput, calls=%fused_computation.35 | convolution fusion | flops 26856652800 | bytes 41156608 | tf_op jit(solution)/vmap(transpose(jvp()))/dot_general | solution.py:9
  559.9 44.6 %fusion.51 = f32[1,1024,3200]{2,1,0:T(8,128)} fusion(bf16[4096,3200]{1,0:T(8,128)(2,1)} %convolution_convert_fusion, f32[4096,3200]{1,0:T(8,128)} %fusion.104, bf16[1,4096,1024]{1,2,0:T(8,128)(2,1)} %copy, f32[4096]{0:T(1024)S(1)} %copy-done.13), kind=kOutput, calls=%fused_computation.66 | convolution fusion | flops 26934771712 | bytes 100155392 | tf_op jit(solution)/vmap(transpose(jvp()))/dot_general | solution.py:21
  604.5 0.1 reduce-scatter.25.cloned.1.call-update
  604.6 0.1 reduce-scatter.23.cloned.1.call-start
  604.7 0.6 copy-done.11
  605.3 45.0 %fusion.45 = f32[1,1024,3200]{2,1,0:T(8,128)} fusion(bf16[4096,3200]{1,0:T(8,128)(2,1)} %convolution_convert_fusion.1, f32[4096,3200]{1,0:T(8,128)} %fusion.92, bf16[1,1,4096,1024]{2,3,1,0:T(8,128)(2,1)} %get-tuple-element.10, f32[4096]{0:T(1024)S(1)} %bitcast.388), kind=kOutput, calls=%fused_computation.64 | convolution fusion | flops 26934771712 | bytes 100155392 | tf_op jit(solution)/vmap(transpose(jvp()))/dot_general | solution.py:21
  650.3 0.1 reduce-scatter.21.cloned.1.call-start
  650.4 50.9 %fusion.48 = f32[1,1024,3200]{2,1,0:T(8,128)} fusion(f32[4096,3200]{1,0:T(8,128)} %fusion.104, f32[4096,3200]{1,0:T(8,128)} %fusion.102, bf16[4096,3200]{1,0:T(8,128)(2,1)} %convolution_convert_fusion, bf16[1,4096,1024]{1,2,0:T(8,128)(2,1)} %copy, f32[4096]{0:T(1024)S(1)} %copy-done.13), kind=kOutput, calls=%fused_computation.65 | convolution fusion | flops 27000307712 | bytes 152584192 | tf_op jit(solution)/vmap(transpose(jvp()))/dot_general | solution.py:20
  701.3 0.1 reduce-scatter.19.cloned.1.call-start
  701.4 37.2 %convolution_bitcast_fusion.1 = f32[1,1024,3200]{2,1,0:T(8,128)} fusion(bf16[4096,3200]{1,0:T(8,128)(2,1)} %fusion.6, bf16[1,1,4096,1024]{2,3,1,0:T(8,128)(2,1)} %get-tuple-element.10, f32[4096]{0:T(1024)S(1)} %bitcast.389), kind=kOutput, calls=%fused_computation.68 | convolution fusion | flops 26856128512 | bytes 47726592 | tf_op jit(solution)/vmap(transpose(jvp()))/dot_general | solution.py:20
  738.7 0.1 all-gather.14.cloned.1.call-start
  738.8 0.5 copy-done.14
  739.3 0.6 dynamic-slice
  740.6 2.2 convert_bitcast_fusion.3
  742.8 2.7 convert_bitcast_fusion.4
  745.5 1.2 copy-done.3
  746.7 2.3 fusion.78
  749.0 80.9 %reduce-scatter.25.cloned.1.call-done = f32[1,256,3200]{2,1,0:T(8,128)} async-done(((f32[1,1024,3200]{2,1,0:T(8,128)}), f32[1,256,3200]{2,1,0:T(8,128)}) %reduce-scatter.25.cloned.1.call-update) | async-done | bytes 3276816
  829.8 2.1 convert_bitcast_fusion.5
  831.9 114.5 %reduce-scatter.23.cloned.1.call-done = f32[1,256,3200]{2,1,0:T(8,128)} async-done(((f32[1,1024,3200]{2,1,0:T(8,128)}), f32[1,256,3200]{2,1,0:T(8,128)}) %reduce-scatter.23.cloned.1.call-update) | async-done | bytes 3276816
  946.5 2.1 convert_bitcast_fusion.6
  948.6 1.2 copy-done.1
  949.7 2.3 fusion.77
  952.0 111.6 %reduce-scatter.21.cloned.1.call-done = f32[1,256,3200]{2,1,0:T(8,128)} async-done(((f32[1,1024,3200]{2,1,0:T(8,128)}), f32[1,256,3200]{2,1,0:T(8,128)}) %reduce-scatter.21.cloned.1.call-update) | async-done | bytes 3276816
  1063.7 2.1 convert_bitcast_fusion.7
  1065.8 115.1 %reduce-scatter.19.cloned.1.call-done = f32[1,256,3200]{2,1,0:T(8,128)} async-done(((f32[1,1024,3200]{2,1,0:T(8,128)}), f32[1,256,3200]{2,1,0:T(8,128)}) %reduce-scatter.19.cloned.1.call-update) | async-done | bytes 3276816
  1180.9 2.1 convert_bitcast_fusion.8
  1183.0 1.2 copy-done
  1184.1 2.3 fusion.76
  1188.4 9.7 all-reduce.16
  1198.7 11.8 fusion.124
  1210.6 0.1 all-gather.12.cloned.1.call-start
  1210.7 11.7 fusion.125
  1222.5 0.1 all-gather.10.cloned.1.call-start
  1222.5 11.3 fusion.126
  1233.9 95.9 %all-gather.14.cloned.1.call-done = bf16[1,2,3200,1024]{3,2,1,0:T(8,128)(2,1)} async-done(((bf16[1,2,800,1024]{3,2,1,0:T(8,128)(2,1)}), bf16[1,2,3200,1024]{3,2,1,0:T(8,128)(2,1)}) %all-gather.14.cloned.1.call-update) | async-done | bytes 13107216 | tf_op jit(solution)/reshape | solution.py:58
  1329.8 122.6 %all-gather.12.cloned.1.call-done = bf16[1,2,1024,3200]{3,2,1,0:T(8,128)(2,1)} async-done(((bf16[1,2,256,3200]{3,2,1,0:T(8,128)(2,1)}), bf16[1,2,1024,3200]{3,2,1,0:T(8,128)(2,1)}) %all-gather.12.cloned.1.call-update) | async-done | bytes 13107216 | tf_op jit(solution)/reshape | solution.py:58
  1452.4 122.6 %all-gather.10.cloned.1.call-done = bf16[1,2,1024,3200]{3,2,1,0:T(8,128)(2,1)} async-done(((bf16[1,2,256,3200]{3,2,1,0:T(8,128)(2,1)}), bf16[1,2,1024,3200]{3,2,1,0:T(8,128)(2,1)}) %all-gather.10.cloned.1.call-update) | async-done | bytes 13107216 | tf_op jit(solution)/reshape | solution.py:58
  1574.9 12.7 copy.5
  1587.7 6.6 copy.6
  1594.3 1.2 slice-done.1
  1595.5 1.3 slice-done.2
  1596.8 4.9 copy.7
  (62 shorter events, 0.7 us)
Async XLA Ops:
  7.2 733.4 %reduce-scatter.29.cloned.1.call-start = ((), (), s32[]{:S(2)}) async-start(), calls=%async_computation.14 | async-start | bytes 16384000
  12.3 49.5 %slice-start.4 = ((s8[13107200]{0:T(1024)(128)(4,1)}), s8[524288]{0:T(1024)(128)(4,1)S(1)}, s32[]{:S(2)}) async-start(s8[13107200]{0:T(1024)(128)(4,1)} %bitcast.378), calls=%async_computation.19 | async-start | bytes 1048576
  24.3 37.5 %copy-start.12 = (f32[4096]{0:T(1024)}, f32[4096]{0:T(1024)S(1)}, u32[]{:S(2)}) copy-start(f32[4096]{0:T(1024)S(1)} %add_rsqrt_fusion) | copy-start | bytes 49156
  24.4 37.5 %slice-start.5 = ((s8[13107200]{0:T(1024)(128)(4,1)}), s8[4194304]{0:T(1024)(128)(4,1)S(1)}, s32[]{:S(2)}) async-start(s8[13107200]{0:T(1024)(128)(4,1)} %bitcast.378), calls=%async_computation.20 | async-start | bytes 8388608
  24.4 37.5 %slice-start.6 = ((s8[13107200]{0:T(1024)(128)(4,1)}), s8[4194304]{0:T(1024)(128)(4,1)S(1)}, s32[]{:S(2)}) async-start(s8[13107200]{0:T(1024)(128)(4,1)} %bitcast.378), calls=%async_computation.21 | async-start | bytes 8388608
  24.4 37.5 %slice-start.7 = ((s8[13107200]{0:T(1024)(128)(4,1)}), s8[4194304]{0:T(1024)(128)(4,1)S(1)}, s32[]{:S(2)}) async-start(s8[13107200]{0:T(1024)(128)(4,1)} %bitcast.378), calls=%async_computation.22 | async-start | bytes 8388608
  177.1 0.6 copy-start.7
  177.1 38.4 %copy-start.9 = (f32[1,1,4096]{2,1,0:T(1,128)}, f32[1,1,4096]{2,1,0:T(1,128)S(1)}, u32[]{:S(2)}) copy-start(f32[1,1,4096]{2,1,0:T(1,128)S(1)} %rsqrt.38) | copy-start | bytes 49156
  177.7 37.8 %copy-start.5 = (bf16[1,1,4096,1024]{2,3,1,0:T(8,128)(2,1)S(1)}, bf16[1,1,4096,1024]{2,3,1,0:T(8,128)(2,1)}, u32[]{:S(2)}) copy-start(bf16[1,1,4096,1024]{2,3,1,0:T(8,128)(2,1)} %get-tuple-element.10) | copy-start | bytes 25165828
  289.0 65.3 %slice-start.8 = ((s8[13107200]{0:T(1024)(128)(4,1)}), s8[524288]{0:T(1024)(128)(4,1)S(1)}, s32[]{:S(2)}) async-start(s8[13107200]{0:T(1024)(128)(4,1)} %bitcast.380), calls=%async_computation.23 | async-start | bytes 1048576
  301.0 53.3 %slice-start.9 = ((s8[13107200]{0:T(1024)(128)(4,1)}), s8[4194304]{0:T(1024)(128)(4,1)S(1)}, s32[]{:S(2)}) async-start(s8[13107200]{0:T(1024)(128)(4,1)} %bitcast.380), calls=%async_computation.24 | async-start | bytes 8388608
  301.0 53.3 %slice-start.10 = ((s8[13107200]{0:T(1024)(128)(4,1)}), s8[4194304]{0:T(1024)(128)(4,1)S(1)}, s32[]{:S(2)}) async-start(s8[13107200]{0:T(1024)(128)(4,1)} %bitcast.380), calls=%async_computation.25 | async-start | bytes 8388608
  301.0 53.3 %slice-start.11 = ((s8[13107200]{0:T(1024)(128)(4,1)}), s8[4194304]{0:T(1024)(128)(4,1)S(1)}, s32[]{:S(2)}) async-start(s8[13107200]{0:T(1024)(128)(4,1)} %bitcast.380), calls=%async_computation.26 | async-start | bytes 8388608
  387.9 43.4 %copy-start.8 = (f32[4096]{0:T(1024)S(1)}, f32[4096]{0:T(1024)}, u32[]{:S(2)}) copy-start(f32[4096]{0:T(1024)} %copy-done.7) | copy-start | bytes 49156
  387.9 43.4 %copy-start.10 = (f32[1,1,4096]{2,1,0:T(1,128)S(1)}, f32[1,1,4096]{2,1,0:T(1,128)}, u32[]{:S(2)}) copy-start(f32[1,1,4096]{2,1,0:T(1,128)} %copy-done.9) | copy-start | bytes 49156
  442.2 3.4 copy-start.6
  478.0 264.8 %reduce-scatter.27.cloned.1.call-start = ((), (), s32[]{:S(2)}) async-start(), calls=%async_computation.13 | async-start | bytes 16384000
  524.2 35.6 %copy-start.13 = (f32[4096]{0:T(1024)S(1)}, f32[4096]{0:T(1024)}, u32[]{:S(2)}) copy-start(f32[4096]{0:T(1024)} %copy-done.12) | copy-start | bytes 49156
  524.3 305.6 %reduce-scatter.25.cloned.1.call-start = ((), (), s32[]{:S(2)}) async-start(), calls=%async_computation.12 | async-start | bytes 16384000
  604.5 0.7 copy-start.11
  604.6 341.9 %reduce-scatter.23.cloned.1.call-start = ((), (), s32[]{:S(2)}) async-start(), calls=%async_computation.11 | async-start | bytes 16384000
  650.3 413.3 %reduce-scatter.21.cloned.1.call-start = ((), (), s32[]{:S(2)}) async-start(), calls=%async_computation.10 | async-start | bytes 16384000
  701.3 479.5 %reduce-scatter.19.cloned.1.call-start = ((), (), s32[]{:S(2)}) async-start(), calls=%async_computation.9 | async-start | bytes 16384000
  738.6 0.7 copy-start.14
  738.7 591.1 %all-gather.14.cloned.1.call-start = ((), (), s32[]{:S(2)}) async-start(), calls=%async_computation.8 | async-start | bytes 16384000 | tf_op jit(solution)/reshape | solution.py:58
  742.7 205.8 %copy-start.2 = (bf16[1,1,800,1024]{3,2,1,0:T(8,128)(2,1)}, bf16[1,1,800,1024]{3,2,1,0:T(8,128)(2,1)S(1)}, u32[]{:S(2)}) copy-start(bf16[1,1,800,1024]{3,2,1,0:T(8,128)(2,1)S(1)} %convert_bitcast_fusion.3) | copy-start | bytes 4915204
  745.5 1.2 copy-start.3
  948.6 1.2 copy-start.1
  1183.0 1.2 copy-start
  1210.6 241.7 %all-gather.12.cloned.1.call-start = ((), (), s32[]{:S(2)}) async-start(), calls=%async_computation.7 | async-start | bytes 16384000 | tf_op jit(solution)/reshape | solution.py:58
  1222.5 352.5 %all-gather.10.cloned.1.call-start = ((), (), s32[]{:S(2)}) async-start(), calls=%async_computation.6 | async-start | bytes 16384000 | tf_op jit(solution)/reshape | solution.py:58
  1574.9 12.7 copy-start.4
  1574.9 19.4 %slice-start = ((s8[13107200]{0:T(1024)(128)(4,1)}), s8[4194304]{0:T(1024)(128)(4,1)S(1)}, s32[]{:S(2)}) async-start(s8[13107200]{0:T(1024)(128)(4,1)} %bitcast.373), calls=%async_computation.15 | async-start | bytes 8388608
  1574.9 20.5 %slice-start.1 = ((s8[13107200]{0:T(1024)(128)(4,1)}), s8[4194304]{0:T(1024)(128)(4,1)S(1)}, s32[]{:S(2)}) async-start(s8[13107200]{0:T(1024)(128)(4,1)} %bitcast.373), calls=%async_computation.16 | async-start | bytes 8388608
  1587.7 9.1 slice-start.2
  1587.7 9.1 slice-start.3
Sparse Core Ops, SparseCore 0:
  478.1 117.5 reduce-scatter.28
  598.1 114.3 reduce-scatter.26
  715.4 114.3 reduce-scatter.24
  832.1 114.3 reduce-scatter.22
  949.2 114.3 reduce-scatter.20
  1066.4 114.3 reduce-scatter.18
  1210.8 118.9 all-gather.13
  1331.9 120.4 all-gather.11
  1454.5 120.4 all-gather.9
where the time goes:
time: 1620 us; the launch traced here: 1610 us
  waiting for transfers between devices  764 us (47%)
  matrix products  590 us (36%)
  other arithmetic  167 us (10%)
  local copies, waits for them, and re-layouts  59.9 us (4%)
  between operations  17.7 us (1%)
    unnamed x15, waiting for transfers between devices  423 us
    reshape x3, waiting for transfers between devices, step(): t.reshape(-1, *t.shape[2:])  341 us
    dot_general x5, matrix products, layer(): up = jnp.dot(a, w['w_up'], preferred_element_type=jnp.float32)  205 us
    dot_general x5, matrix products, layer(): gate = jnp.dot(a, w['w_gate'], preferred_element_type=jnp.float32)  197 us
    dot_general x5, matrix products, matmul(): jnp.dot(a, w, preferred_element_type=jnp.float32).astype(jnp.bfloat16)  188 us
    unnamed x6, other arithmetic  106 us
    unnamed x59, local copies, waits for them, and re-layouts  59.3 us
    reshape x3, other arithmetic, step(): t.reshape(-1, *t.shape[2:])  34.8 us
  transfers between devices with their start and end apart: 9, of which 7 were waited for; matrix products, arithmetic and copies ran while one was open for 19% of the time, Pallas kernels for 0%

commit v1 on v0

v1 whole, which is shorter than its diff:
```python
import functools
import jax, jax.numpy as jnp
from jax import lax
from jax.experimental import pallas as pl
from jax.experimental.pallas import tpu as pltpu
from jax.sharding import PartitionSpec as P

F32, BF16 = jnp.float32, jnp.bfloat16
def dot(a, b): return jnp.dot(a, b, preferred_element_type=F32)
def dot_nt(a, b): return lax.dot_general(a, b, (((1,), (1,)), ((), ())), preferred_element_type=F32)
def sigmoid(x): return 0.5 * jnp.tanh(0.5 * x) + 0.5

def fwd_kernel(chunk, with_down, h_ref, wg_ref, wu_ref, *refs):
    if with_down: wd_ref, aT_ref, gate_ref, up_ref, actT_ref, h1_ref, a_ref, act_ref, wt_ref = refs
    else: aT_ref, gate_ref, up_ref, actT_ref, a_ref, wt_ref = refs
    ff = wg_ref.shape[1]; full = ff // chunk; tail = ff - full * chunk
    @pl.when(pl.program_id(0) == 0)
    def _():
        wt_ref[:, :tail] = wg_ref[:, full*chunk:]; wt_ref[:, tail:] = wu_ref[:, full*chunk:]
    wide = h_ref[...].astype(F32)
    scale = lax.rsqrt(jnp.mean(wide * wide, -1, keepdims=True) + 1e-6)
    a = (wide * scale).astype(BF16)
    a_ref[...] = a
    aT_ref[...] = a.T
    def part(g, u, cols):
        gate_ref[:, cols] = g; up_ref[:, cols] = u
        act = (g * sigmoid(g) * u).astype(BF16)
        if with_down: act_ref[:, cols] = act
        actT_ref[cols, :] = act.T
    for c in range(full):
        cols = pl.ds(c * chunk, chunk)
        part(dot(a_ref[...], wg_ref[:, cols]), dot(a_ref[...], wu_ref[:, cols]), cols)
    gu = dot(a_ref[...], wt_ref[...])
    part(gu[:, :tail], gu[:, tail:], pl.ds(full*chunk, tail))
    if with_down:
        o = dot(act_ref[...], wd_ref[...]).astype(BF16)
        h1_ref[...] = h_ref[...] + o

def fwd(layer, h, wg, wu, wd=None, tb=256, chunk=512):
    t, d = h.shape; ff = wg.shape[2]
    once = pl.Buffered(1)
    w_spec = lambda: pl.BlockSpec((None, d, ff), lambda i: (layer, 0, 0), pipeline_mode=once)
    ins = [h, wg, wu]; in_specs = [pl.BlockSpec((tb, d), lambda i: (i, 0)), w_spec(), w_spec()]
    outs = [((d, t), BF16, (d, tb), lambda i: (0, i)), ((t, ff), F32, (tb, ff), lambda i: (i, 0)), ((t, ff), F32, (tb, ff), lambda i: (i, 0)),
            ((ff, t), BF16, (ff, tb), lambda i: (0, i))]
    scratch = [pltpu.VMEM((tb, d), BF16)]
    tail = ff % chunk
    if wd is not None:
        ins.append(wd); in_specs.append(pl.BlockSpec((None, ff, d), lambda i: (layer, 0, 0), pipeline_mode=once))
        outs.append(((t, d), BF16, (tb, d), lambda i: (i, 0)))
        scratch.append(pltpu.VMEM((tb, ff), BF16))
    scratch.append(pltpu.VMEM((d, 2 * tail), BF16))
    n = 3 if wd is not None else 2
    return pl.pallas_call(functools.partial(fwd_kernel, chunk, wd is not None), grid=(t // tb,),
        in_specs=in_specs, out_specs=[pl.BlockSpec(b, m) for _, _, b, m in outs],
        out_shape=[jax.ShapeDtypeStruct(s, dt) for s, dt, _, _ in outs], scratch_shapes=scratch,
        compiler_params=pltpu.CompilerParams(vmem_limit_bytes=61 << 20, dimension_semantics=("arbitrary",)),
        cost_estimate=pl.CostEstimate(flops=2*n*t*d*ff, bytes_accessed=2*n*d*ff+t*ff*10+t*d*6, transcendentals=t*ff), name=f"fwd{layer}")(*ins)

def dwd_kernel(actT_ref, dh_ref, after_ref, o_ref):
    o_ref[...] = dot(actT_ref[...], dh_ref[...]).astype(BF16)

def dwd(actT, dh, after, rb=640, cb=1024):
    ff, t = actT.shape; d = dh.shape[1]
    return pl.pallas_call(dwd_kernel, grid=(d // cb, ff // rb),
        in_specs=[pl.BlockSpec((rb, t), lambda c, r: (r, 0)), pl.BlockSpec((t, cb), lambda c, r: (0, c), pipeline_mode=pl.Buffered(1) if cb == d else None), pl.BlockSpec(memory_space=pl.ANY)],
        out_specs=pl.BlockSpec((rb, cb), lambda c, r: (r, c)), out_shape=jax.ShapeDtypeStruct((ff, d), BF16),
        compiler_params=pltpu.CompilerParams(vmem_limit_bytes=60 << 20, dimension_semantics=("arbitrary","arbitrary")),
        cost_estimate=pl.CostEstimate(flops=2*t*d*ff, bytes_accessed=2*(t*ff+t*d+d*ff), transcendentals=0), name="dwd")(actT, dh, after)

def bwd_kernel(J, nt, ff, sub, keep, gate_ref, up_ref, dh_ref, wd_ref, aT_ref, after_ref, dw_ref, *refs):
    if keep: dgo_ref, duo_ref, dg0, du0, dg1, du1 = refs
    else: dg0, du0, dg1, du1 = refs
    j, t = pl.program_id(0), pl.program_id(1)
    tt = gate_ref.shape[0]
    nfull, tail = ff // J, ff % J
    d = aT_ref.shape[0]; q = d // nt
    rows = pl.ds(pl.multiple_of(t * q, q), q)
    def stage_a(w, put):
        cols = pl.ds(0, w)
        for r in range(tt // sub):
            rs = pl.ds(r * sub, sub)
            dst = pl.ds(pl.multiple_of(t * tt + r * sub, sub), sub)
            dact = dot_nt(dh_ref[rs, :], wd_ref[cols, :]).astype(BF16).astype(F32)
            g = gate_ref[rs, cols]; u = up_ref[rs, cols]
            s = sigmoid(g); silu = g * s
            dup = (dact * silu).astype(BF16)
            dgate = (dact * u * (s + silu * (1.0 - s))).astype(BF16)
            put(dst, dgate, dup)
            if keep: dgo_ref[rs, cols] = dgate; duo_ref[rs, cols] = dup
    def a_full(dg, du):
        def put(dst, a, b): dg[dst, :] = a; du[dst, :] = b
        stage_a(J, put)
    def a_tail(dg):
        def put(dst, a, b): dg[dst, :tail] = a; dg[dst, tail:2*tail] = b
        stage_a(tail, put)
    def b_full(dg, du):
        dw_ref[0] = dot(aT_ref[rows, :], dg[...]).astype(BF16)
        dw_ref[1] = dot(aT_ref[rows, :], du[...]).astype(BF16)
    def b_tail(dg):
        o = dot(aT_ref[rows, :], dg[:, :2*tail]).astype(BF16)
        dw_ref[0, :, :tail] = o[:, :tail]; dw_ref[1, :, :tail] = o[:, tail:]
    odd = lax.rem(j, 2) == 1
    assert nfull % 2 == 0
    @pl.when(j == 0)
    def _(): a_full(dg0, du0)
    @pl.when(odd & (j < nfull))
    def _(): a_full(dg1, du1); b_full(dg0, du0)
    @pl.when(~odd & (j > 0) & (j < nfull))
    def _(): a_full(dg0, du0); b_full(dg1, du1)
    @pl.when(j == nfull)
    def _(): a_tail(dg0); b_full(dg1, du1)
    @pl.when(j == nfull + 1)
    def _(): b_tail(dg0)

def bwd(layer, gate, up, dh, wd, aT, after, J=512, tt=1024, sub=512, keep=True):
    t, ff = gate.shape; d = dh.shape[1]; nt = t // tt; nj = -(-ff // J)
    once = pl.Buffered(1)
    jj = lambda j: jnp.minimum(j, nj - 1)
    ti = lambda j, i: jnp.where(j == nj, nt - 1, i)
    tile = pl.BlockSpec((tt, J), lambda j, i: (ti(j, i), jj(j)))
    in_specs = [tile, tile, pl.BlockSpec((tt, d), lambda j, i: (ti(j, i), 0)), pl.BlockSpec((None, J, d), lambda j, i: (layer, jj(j), 0)),
        pl.BlockSpec((d, t), lambda j, i: (0, 0), pipeline_mode=once), pl.BlockSpec(memory_space=pl.ANY)]
    out_specs = [pl.BlockSpec((2, d // nt, J), lambda j, i: (0, jnp.where(j == 0, 0, i), jnp.maximum(j - 1, 0)))] + [tile] * (2 * keep)
    out_shape = [jax.ShapeDtypeStruct((2, d, ff), BF16)] + [jax.ShapeDtypeStruct((t, ff), BF16)] * (2 * keep)
    return pl.pallas_call(functools.partial(bwd_kernel, J, nt, ff, sub, keep), grid=(nj + 1, nt), in_specs=in_specs,
        out_specs=out_specs, out_shape=out_shape, scratch_shapes=[pltpu.VMEM((t, J), BF16)] * 4,
        compiler_params=pltpu.CompilerParams(vmem_limit_bytes=61 << 20, dimension_semantics=("arbitrary", "arbitrary")),
        cost_estimate=pl.CostEstimate(flops=6*t*d*ff, bytes_accessed=8*t*ff, transcendentals=t*ff), name=f"bwd{layer}")(gate, up, dh, wd, aT, after)

def dx_kernel(n, sub, dg_ref, du_ref, wg_ref, wu_ref, h_ref, dh_ref, o_ref, da_ref):
    i = pl.program_id(0)
    def epi(rs):
        da = da_ref[rs, :].astype(BF16).astype(F32)
        wide = h_ref[rs, :].astype(F32)
        scale = lax.rsqrt(jnp.mean(wide * wide, -1, keepdims=True) + 1e-6)
        mean = jnp.mean(da * wide, -1, keepdims=True)
        dw = da * scale - wide * (scale * scale * scale * mean)
        o_ref[rs, :] = dh_ref[rs, :] + dw.astype(BF16)
    def mm(rs): da_ref[rs, :] = dot_nt(dg_ref[rs, :], wg_ref[...]) + dot_nt(du_ref[rs, :], wu_ref[...])
    blocks = [pl.ds(r * sub, sub) for r in range(dg_ref.shape[0] // sub)]
    @pl.when(i == 0)
    def _():
        for rs in blocks: mm(rs)
    @pl.when((i > 0) & (i < n))
    def _():
        for rs in blocks: epi(rs); mm(rs)
    @pl.when(i == n)
    def _():
        for rs in blocks: epi(rs)

def dx(layer, dg, du, wg, wu, h, dh, tb=512, sub=512):
    t, ff = dg.shape; d = dh.shape[1]; once = pl.Buffered(1); n = t // tb
    cur = lambda i: (jnp.minimum(i, n - 1), 0)
    prv = lambda i: (jnp.maximum(i - 1, 0), 0)
    w_spec = pl.BlockSpec((None, d, ff), lambda i: (layer, 0, 0), pipeline_mode=once)
    return pl.pallas_call(functools.partial(dx_kernel, n, sub), grid=(n + 1,),
        in_specs=[pl.BlockSpec((tb, ff), cur), pl.BlockSpec((tb, ff), cur), w_spec, w_spec, pl.BlockSpec((tb, d), prv), pl.BlockSpec((tb, d), prv)],
        out_specs=pl.BlockSpec((tb, d), prv), out_shape=jax.ShapeDtypeStruct((t, d), BF16), scratch_shapes=[pltpu.VMEM((tb, d), F32)],
        compiler_params=pltpu.CompilerParams(vmem_limit_bytes=60 << 20, dimension_semantics=("arbitrary",)),
        cost_estimate=pl.CostEstimate(flops=4*t*d*ff, bytes_accessed=4*t*ff, transcendentals=0), name=f"dx{layer}")(dg, du, wg, wu, h, dh)

def place_kernel(own_ref, left_ref, right_ref, far0_ref, far1_ref, out_ref, send):
    k = pl.program_id(0)

    @pl.when(k == 0)
    def _():
        out_ref[...] = own_ref[...]

    @pl.when(k == 1)
    def _():
        out_ref[...] = left_ref[...]

    @pl.when(k == 2)
    def _():
        out_ref[...] = right_ref[...]

    @pl.when(k == 3)
    def _():
        out_ref[0] = far0_ref[...]
        out_ref[1] = far1_ref[...]


def place(me, n, own, left, right, far0, far1):
    layers, rows, cols = own.shape
    where = (me + jnp.array([0, n - 1, 1, 2], jnp.int32)) % n

    def body(where_ref, *refs):
        place_kernel(*refs, None)

    def whole(k, where_ref):
        return (0, 0, 0)

    three = pl.BlockSpec((layers, rows, cols), whole)
    two = pl.BlockSpec((rows, cols), lambda k, where_ref: (0, 0))
    return pl.pallas_call(
        body,
        grid_spec=pltpu.PrefetchScalarGridSpec(
            num_scalar_prefetch=1,
            grid=(n,),
            in_specs=[three, three, three, two, two],
            out_specs=pl.BlockSpec((layers, rows, cols), lambda k, where_ref: (0, where_ref[k], 0)),
        ),
        out_shape=jax.ShapeDtypeStruct((layers, n * rows, cols), own.dtype),
        compiler_params=pltpu.CompilerParams(vmem_limit_bytes=40 << 20, dimension_semantics=("arbitrary",)),
        cost_estimate=pl.CostEstimate(flops=0, bytes_accessed=4 * layers * n * rows * cols, transcendentals=0),
        name="place",
    )(where, own, left, right, far0, far1)


def gathered(own, n):
    to_right = [(i, (i + 1) % n) for i in range(n)]
    to_left = [(i, (i - 1) % n) for i in range(n)]
    left = lax.ppermute(own, "dp", to_right)
    right = lax.ppermute(own, "dp", to_left)
    far0 = lax.ppermute(left[0], "dp", to_right)
    far1 = lax.ppermute(right[1], "dp", to_left)
    return place(lax.axis_index("dp"), n, own, left, right, far0, far1)


def adamw(w, m, v, g):
    m = 0.9 * m + 0.1 * g
    v = 0.95 * v + 0.05 * g * g
    step = m * lax.rsqrt(v + 1e-8) + 0.1 * w
    return (w - 0.02 * step).astype(BF16), m, v


def solution(mesh):
    n = mesh.shape["dp"]

    def of_a_device(x, dy, wg, wu, wd, *moments):
        x, dy = x[0], dy[0]
        m, v = moments[:3], moments[3:]
        a0, g0, u0, act0, h1 = fwd(0, x, wg, wu, wd)
        a1, g1, u1, act1 = fwd(1, h1, wg, wu)

        def scattered(t):
            return lax.psum_scatter(t, "dp", scatter_dimension=t.ndim - 2, tiled=True)

        mine = dwd(act1, dy, act1, rb=800)
        dwd1 = scattered(mine)
        dgu1, dg, du = bwd(1, g1, u1, dy, wd, a1, mine, sub=256, keep=True)
        dgu1 = scattered(dgu1)
        dh = dx(1, dg, du, wg, wu, h1, dy)
        mine = dwd(act0, dh, dwd1, rb=800)
        dwd0 = scattered(mine)
        dgu0, = bwd(0, g0, u0, dh, wd, a0, dgu1, sub=256, keep=False)
        dgu0 = scattered(dgu0)
        grads = [jnp.stack(p).astype(F32) for p in ((dgu0[0], dgu1[0]), (dgu0[1], dgu1[1]), (dwd0, dwd1))]
        total = lax.psum(sum(jnp.sum(g * g) for g in grads), "dp")
        count = sum(w.size for w in (wg, wu, wd))
        factor = jnp.minimum(1.0, 0.5 * lax.rsqrt(total / count + 1e-30))
        me = lax.axis_index("dp")
        new = []
        for w, mm, vv, g in zip((wg, wu, wd), m, v, grads):
            rows = g.shape[1]
            own = lax.dynamic_slice_in_dim(w, me * rows, rows, 1)
            new.append(adamw(own.astype(F32), mm, vv, g * factor))
        return tuple(gathered(one[0], n) for one in new) + tuple(one[1] for one in new) + tuple(one[2] for one in new)

    seq = P(("rep", "dp"))
    whole, rows = P(), P(None, "dp")
    return jax.shard_map(
        of_a_device,
        mesh=mesh,
        in_specs=(seq, seq) + (whole,) * 3 + (rows,) * 6,
        out_specs=(P("rep"),) * 3 + (P("rep", "dp"),) * 6,
        check_vma=False,
    )
```

time: 1620 us -> 1040 us (0.64)
  matrix products: 590 us -> 0 us
  Pallas kernels: 0 us -> 563 us
  waiting for transfers between devices: 764 us -> 376 us
  other arithmetic: 167 us -> 38.1 us
  local copies, waits for them, and re-layouts: 59.9 us -> 18.5 us
    dot_general x15 -> x0, matrix products: 590 us -> none  [the longest x5 205 us: layer(): up = jnp.dot(a, w['w_up'], preferred_element_type=jnp.float32)]
    pallas_call x0 -> x10, Pallas kernels: none -> 563 us  [the longest x2 235 us: bwd(): pl.pallas_call(functools.partial(bwd_kernel, J, nt, ff, sub, keep), grid=...]
    unnamed x15 -> x4, waiting for transfers between devices: 423 us -> 0.21 us
    reshape x3 -> x0, waiting for transfers between devices: 341 us -> none  [step(): t.reshape(-1, *t.shape[2:])]
    ppermute x0 -> x12, waiting for transfers between devices: none -> 257 us  [the longest x3 178 us: gathered(): left = lax.ppermute(own, 'dp', to_right)]
    reduce_scatter x0 -> x4, waiting for transfers between devices: none -> 119 us  [scattered(): return lax.psum_scatter(t, 'dp', scatter_dimension=t.ndim - 2, tiled=True)]
    unnamed x6 -> x0, other arithmetic: 106 us -> none
    unnamed x59 -> x32, local copies, waits for them, and re-layouts: 59.3 us -> 4.46 us
  transfers between devices with their start and end apart: 9 -> 16, of which waited for: 7 -> 8; matrix products, arithmetic and copies ran while one was open for 19% -> 4% of each run, Pallas kernels for 0% -> 34%
where the time goes in v1:
time: 1040 us
  Pallas kernels  563 us (54%)
  waiting for transfers between devices  376 us (36%)
  other arithmetic  38.1 us (4%)
  local copies, waits for them, and re-layouts  18.5 us (2%)
  between operations  17 us (2%)
  starting transfers between devices  13.4 us (1%)
    pallas_call x2, Pallas kernels, bwd(): pl.pallas_call(functools.partial(bwd_kernel, J, nt, ff, sub, keep), grid=...  235 us
    ppermute x3, waiting for transfers between devices, gathered(): left = lax.ppermute(own, 'dp', to_right)  178 us
    pallas_call x2, Pallas kernels, fwd(): pl.pallas_call(functools.partial(fwd_kernel, chunk, wd is not None), grid...  165 us
    reduce_scatter x4, waiting for transfers between devices, scattered(): return lax.psum_scatter(t, 'dp', scatter_dimension=t.ndim - 2, tiled=True)  119 us
    ppermute x3, waiting for transfers between devices, gathered(): far0 = lax.ppermute(left[0], 'dp', to_right)  78.9 us
    pallas_call x1, Pallas kernels, dx(): pl.pallas_call(functools.partial(dx_kernel, n, sub), grid=(n + 1,), in_sp...  70.6 us
    pallas_call x2, Pallas kernels, dwd(): pl.pallas_call(dwd_kernel, grid=(d // cb, ff // rb), in_specs=[pl.BlockSp...  68.2 us
    convert_element_type x3, other arithmetic, adamw(): return ((w - 0.02 * step).astype(BF16), m, v)  31.8 us
  transfers between devices with their start and end apart: 16, of which 8 were waited for; matrix products, arithmetic and copies ran while one was open for 4% of the time, Pallas kernels for 34%

profile of v1, /device:TPU:112, one launch (start us, length us, event | category | flops | bytes accessed | tf_op | source)
XLA Modules:
  0.0 1035.5 jit_solution(10558260708405475735)
XLA Ops:
  7.2 0.1 reduce-scatter.9.cloned.1.call-start
  7.3 96.7 %fwd0.1 = (bf16[1024,4096]{1,0:T(8,128)(2,1)}, f32[4096,3200]{1,0:T(8,128)}, f32[4096,3200]{1,0:T(8,128)}, bf16[3200,4096]{1,0:T(8,128)(2,1)}, bf16[4096,1024]{1,0:T(8,128)(2,1)}) custom-call(bf16[4096,1024]{1,0:T(8,128)(2,1)} %bitcast.20, bf16[2,1024,3200]{2,1,0:T(8,128)(2,1)} %wg_ref.5, bf16[2,1024,3200]{2,1,0:T(8,128)(2,1)} %wu_ref.5, ...), custom_call_target="tpu_custom_call" | custom-call | flops 80530636800 | bytes 175898624 | tf_op jit(solution)/shard_map/fwd0/pallas_call | solution.py:54
  104.0 68.6 %fwd1.1 = (bf16[1024,4096]{1,0:T(8,128)(2,1)}, f32[4096,3200]{1,0:T(8,128)}, f32[4096,3200]{1,0:T(8,128)}, bf16[3200,4096]{1,0:T(8,128)(2,1)}) custom-call(bf16[4096,1024]{1,0:T(8,128)(2,1)} %get-tuple-element.23.h_ref, bf16[2,1024,3200]{2,1,0:T(8,128)(2,1)} %wg_ref.5, bf16[2,1024,3200]{2,1,0:T(8,128)(2,1)} %wu_ref.5), custom_call_target="tpu_custom_call" | custom-call | flops 53687091200 | bytes 169345024 | tf_op jit(solution)/shard_map/fwd1/pallas_call | solution.py:54
  172.6 34.1 %dwd.2.after_ref = bf16[3200,1024]{1,0:T(8,128)(2,1)} custom-call(bf16[3200,4096]{1,0:T(8,128)(2,1)} %get-tuple-element.27.actT_ref.after_ref, bf16[4096,1024]{1,0:T(8,128)(2,1)} %bitcast.21, bf16[3200,4096]{1,0:T(8,128)(2,1)} %get-tuple-element.27.actT_ref.after_ref), custom_call_target="tpu_custom_call" | custom-call | flops 26843545600 | bytes 41156608 | tf_op jit(solution)/shard_map/dwd/pallas_call | solution.py:65
  206.7 0.1 reduce-scatter.9.cloned.1.call-update
  206.8 0.3 reduce-scatter.5.cloned.1.call-start
  207.1 119.9 %bwd1.1 = (bf16[2,1024,3200]{2,1,0:T(8,128)(2,1)}, bf16[4096,3200]{1,0:T(8,128)(2,1)}, bf16[4096,3200]{1,0:T(8,128)(2,1)}) custom-call(f32[4096,3200]{1,0:T(8,128)} %get-tuple-element.24.gate_ref, f32[4096,3200]{1,0:T(8,128)} %get-tuple-element.25.up_ref, bf16[4096,1024]{1,0:T(8,128)(2,1)} %bitcast.22, bf16[2,3200,1024]{2,1,0:T(8,128)(2,1)} %wd_ref.3, ...), custom_call_target="tpu_custom_call" | custom-call | flops 80530636800 | bytes 104857600 | tf_op jit(solution)/shard_map/bwd1/pallas_call | solution.py:126
  326.9 0.1 reduce-scatter.5.cloned.1.call-update
  327.0 0.5 reduce-scatter.11.cloned.1.call-start
  327.5 70.6 %dx1.1.dh_ref = bf16[4096,1024]{1,0:T(8,128)(2,1)} custom-call(bf16[4096,3200]{1,0:T(8,128)(2,1)} %get-tuple-element.28.dg_ref, bf16[4096,3200]{1,0:T(8,128)(2,1)} %get-tuple-element.29.du_ref, bf16[2,1024,3200]{2,1,0:T(8,128)(2,1)} %wg_ref.5, bf16[2,1024,3200]{2,1,0:T(8,128)(2,1)} %wu_ref.5, bf16[4096,1024]{1,0:T(8,128)(2,1)} %get-tuple-element.23.h_ref, ...), custom_call_target="tpu_custom_call" | custom-call | flops 53687091200 | bytes 52428800 | tf_op jit(solution)/shard_map/dx1/pallas_call | solution.py:157
  398.0 34.1 %dwd.3 = bf16[3200,1024]{1,0:T(8,128)(2,1)} custom-call(bf16[3200,4096]{1,0:T(8,128)(2,1)} %get-tuple-element.32.actT_ref, bf16[4096,1024]{1,0:T(8,128)(2,1)} %dx1.1.dh_ref, bf16[800,1024]{1,0:T(8,128)(2,1)} %reduce-scatter.9.cloned.1.call-done.after_ref), custom_call_target="tpu_custom_call" | custom-call | flops 26843545600 | bytes 41156608 | tf_op jit(solution)/shard_map/dwd/pallas_call | solution.py:65
  432.2 0.1 reduce-scatter.11.cloned.1.call-update
  432.2 0.1 reduce-scatter.7.cloned.1.call-start
  432.3 12.4 %reduce-scatter.5.cloned.1.call-done.after_ref = bf16[2,256,3200]{2,1,0:T(8,128)(2,1)} async-done(((bf16[2,1024,3200]{2,1,0:T(8,128)(2,1)}), bf16[2,256,3200]{2,1,0:T(8,128)(2,1)}) %reduce-scatter.5.cloned.1.call-update) | async-done | bytes 3276816 | tf_op jit(solution)/shard_map/reduce_scatter | solution.py:238
  444.7 115.3 %bwd0.1 = bf16[2,1024,3200]{2,1,0:T(8,128)(2,1)} custom-call(f32[4096,3200]{1,0:T(8,128)} %get-tuple-element.21.gate_ref, f32[4096,3200]{1,0:T(8,128)} %get-tuple-element.22.up_ref, bf16[4096,1024]{1,0:T(8,128)(2,1)} %dx1.1.dh_ref, bf16[2,3200,1024]{2,1,0:T(8,128)(2,1)} %wd_ref.3, bf16[1024,4096]{1,0:T(8,128)(2,1)} %get-tuple-element.30.aT_ref, ...), custom_call_target="tpu_custom_call" | custom-call | flops 80530636800 | bytes 104857600 | tf_op jit(solution)/shard_map/bwd0/pallas_call | solution.py:126
  560.0 0.1 reduce-scatter.7.cloned.1.call-update
  560.1 0.0 reduce-scatter.11.cloned.1.call-done
  560.1 1.3 copy-done.14
  561.5 3.7 fusion.11
  565.2 3.3 fusion.29
  568.5 106.1 %reduce-scatter.7.cloned.1.call-done = bf16[2,256,3200]{2,1,0:T(8,128)(2,1)} async-done(((bf16[2,1024,3200]{2,1,0:T(8,128)(2,1)}), bf16[2,256,3200]{2,1,0:T(8,128)(2,1)}) %reduce-scatter.7.cloned.1.call-update) | async-done | bytes 3276816 | tf_op jit(solution)/shard_map/reduce_scatter | solution.py:238
  674.6 2.3 fusion.28
  676.9 0.0 copy-start.8
  676.9 0.0 copy-start.12
  676.9 1.1 copy-done.8
  678.1 2.5 fusion.9
  682.5 9.1 psum.7
  692.4 0.0 copy-start.11
  692.4 0.0 copy-start.13
  692.4 11.1 %fusion.17 = (bf16[2,800,1024]{2,1,0:T(8,128)(2,1)S(1)}, f32[2,800,1024]{2,1,0:T(8,128)}, f32[2,800,1024]{2,1,0:T(8,128)}) fusion(bf16[2,3200,1024]{2,1,0:T(8,128)(2,1)} %wd_ref.3, s32[]{:T(128)S(6)} %select_n.26, f32[]{:T(128)S(6)} %min_shard_map.3, bf16[1,800,1024]{2,1,0:T(8,128)(2,1)S(1)} %bitcast.17, bf16[1,800,1024]{2,1,0:T(8,128)(2,1)} %bitcast.19, ...), kind=kLoop, calls=%fused_computation.32 | loop fusion | flops 32768000 | bytes 36044808 | tf_op jit(solution)/shard_map/convert_element_type | solution.py:225
  703.5 1.2 collective-permute-start.8
  704.6 2.1 collective-permute-start.9
  706.7 10.4 %fusion.14 = (bf16[2,256,3200]{2,1,0:T(8,128)(2,1)S(1)}, f32[2,256,3200]{2,1,0:T(8,128)}, f32[2,256,3200]{2,1,0:T(8,128)}) fusion(bf16[2,1024,3200]{2,1,0:T(8,128)(2,1)} %wu_ref.5, s32[]{:T(128)S(6)} %select_n.23, f32[]{:T(128)S(6)} %min_shard_map.3, bf16[1,256,3200]{2,1,0:T(8,128)(2,1)S(1)} %copy-done.11, bf16[1,256,3200]{2,1,0:T(8,128)(2,1)S(1)} %copy-done.13, ...), kind=kLoop, calls=%fused_computation.29 | loop fusion | flops 32768000 | bytes 36044808 | tf_op jit(solution)/shard_map/convert_element_type | solution.py:225
  717.1 0.1 collective-permute-start.4
  717.2 3.2 collective-permute-start.5
  720.4 10.3 fusion.8
  730.7 47.8 %collective-permute-done.8.refs_1_ = bf16[2,800,1024]{2,1,0:T(8,128)(2,1)S(1)} collective-permute-done((bf16[2,800,1024]{2,1,0:T(8,128)(2,1)S(1)}, bf16[2,800,1024]{2,1,0:T(8,128)(2,1)S(1)}, u32[]{:S(2)}, u32[]{:S(2)}) %collective-permute-start.8) | collective-permute-done | bytes 3276832 | tf_op jit(solution)/shard_map/ppermute | solution.py:214
  778.5 0.1 slice_bitcast_fusion.1
  778.6 2.1 collective-permute-start.10
  780.7 1.6 slice_bitcast_fusion
  782.3 0.0 copy-start.15
  782.3 66.4 %collective-permute-done.4.refs_1_ = bf16[2,256,3200]{2,1,0:T(8,128)(2,1)S(1)} collective-permute-done((bf16[2,256,3200]{2,1,0:T(8,128)(2,1)S(1)}, bf16[2,256,3200]{2,1,0:T(8,128)(2,1)S(1)}, u32[]{:S(2)}, u32[]{:S(2)}) %collective-permute-start.4) | collective-permute-done | bytes 3276832 | tf_op jit(solution)/shard_map/ppermute | solution.py:214
  848.7 0.0 collective-permute-start.11
  848.7 1.4 slice_bitcast_fusion.3
  850.1 0.0 collective-permute-done.5.refs_2_
  850.1 1.9 collective-permute-start.6
  852.0 2.8 slice_bitcast_fusion.2
  854.8 64.2 %collective-permute-done.refs_1_ = bf16[2,256,3200]{2,1,0:T(8,128)(2,1)S(1)} collective-permute-done((bf16[2,256,3200]{2,1,0:T(8,128)(2,1)S(1)}, bf16[2,256,3200]{2,1,0:T(8,128)(2,1)S(1)}, u32[]{:S(2)}, u32[]{:S(2)}) %collective-permute-start) | collective-permute-done | bytes 3276832 | tf_op jit(solution)/shard_map/ppermute | solution.py:214
  918.9 0.0 collective-permute-start.7
  918.9 1.4 slice_bitcast_fusion.5
  920.3 0.0 collective-permute-done.1.refs_2_
  920.3 2.0 collective-permute-start.2
  922.3 1.3 slice_bitcast_fusion.4
  923.6 30.4 %collective-permute-done.10.refs_3_ = bf16[800,1024]{1,0:T(8,128)(2,1)S(1)} collective-permute-done((bf16[800,1024]{1,0:T(8,128)(2,1)S(1)}, bf16[800,1024]{1,0:T(8,128)(2,1)S(1)}, u32[]{:S(2)}, u32[]{:S(2)}) %collective-permute-start.10) | collective-permute-done | bytes 1638432 | tf_op jit(solution)/shard_map/ppermute | solution.py:216
  954.0 0.0 collective-permute-start.3
  954.1 0.0 collective-permute-done.11.refs_4_
  954.1 0.0 copy-start.1
  954.1 1.9 copy-done.1
  956.0 7.8 place.5
  963.9 25.3 %collective-permute-done.6.refs_3_ = bf16[256,3200]{1,0:T(8,128)(2,1)} collective-permute-done((bf16[256,3200]{1,0:T(8,128)(2,1)}, bf16[256,3200]{1,0:T(8,128)(2,1)}, u32[]{:S(2)}, u32[]{:S(2)}) %collective-permute-start.6) | collective-permute-done | bytes 1638432 | tf_op jit(solution)/shard_map/ppermute | solution.py:216
  989.1 8.6 place.4
  997.7 23.2 %collective-permute-done.2.refs_3_ = bf16[256,3200]{1,0:T(8,128)(2,1)} collective-permute-done((bf16[256,3200]{1,0:T(8,128)(2,1)}, bf16[256,3200]{1,0:T(8,128)(2,1)}, u32[]{:S(2)}, u32[]{:S(2)}) %collective-permute-start.2) | collective-permute-done | bytes 1638432 | tf_op jit(solution)/shard_map/ppermute | solution.py:216
  1021.0 0.0 collective-permute-done.3.refs_4_
  1021.0 7.6 place.3
  (29 shorter events, 0.1 us)
Async XLA Ops:
  7.2 390.9 %reduce-scatter.9.cloned.1.call-start = ((), (), s32[]{:S(2)}) async-start(), calls=%async_computation.6 | async-start | bytes 8192000 | tf_op jit(solution)/shard_map/reduce_scatter | solution.py:238
  206.8 237.9 %reduce-scatter.5.cloned.1.call-start = ((), (), s32[]{:S(2)}) async-start(), calls=%async_computation.4 | async-start | bytes 16384000 | tf_op jit(solution)/shard_map/reduce_scatter | solution.py:238
  327.0 233.1 %reduce-scatter.11.cloned.1.call-start = ((), (), s32[]{:S(2)}) async-start(), calls=%async_computation.7 | async-start | bytes 8192000 | tf_op jit(solution)/shard_map/reduce_scatter | solution.py:238
  432.2 242.4 %reduce-scatter.7.cloned.1.call-start = ((), (), s32[]{:S(2)}) async-start(), calls=%async_computation.5 | async-start | bytes 16384000 | tf_op jit(solution)/shard_map/reduce_scatter | solution.py:238
  560.0 1.4 copy-start.14
  674.6 3.4 copy-start.10
  676.9 1.2 copy-start.8
  676.9 3.7 copy-start.12
  692.4 14.4 %copy-start.11 = (bf16[1,256,3200]{2,1,0:T(8,128)(2,1)S(1)}, bf16[1,256,3200]{2,1,0:T(8,128)(2,1)}, u32[]{:S(2)}) copy-start(bf16[1,256,3200]{2,1,0:T(8,128)(2,1)} %get-tuple-element.44) | copy-start | bytes 4915204
  692.4 14.3 %copy-start.13 = (bf16[1,256,3200]{2,1,0:T(8,128)(2,1)S(1)}, bf16[1,256,3200]{2,1,0:T(8,128)(2,1)}, u32[]{:S(2)}) copy-start(bf16[1,256,3200]{2,1,0:T(8,128)(2,1)} %copy-done.12) | copy-start | bytes 4915204
  703.5 16.9 %copy-start.9 = (bf16[1,256,3200]{2,1,0:T(8,128)(2,1)S(1)}, bf16[1,256,3200]{2,1,0:T(8,128)(2,1)}, u32[]{:S(2)}) copy-start(bf16[1,256,3200]{2,1,0:T(8,128)(2,1)} %copy-done.8) | copy-start | bytes 4915204
  703.5 75.0 %collective-permute-start.8 = (bf16[2,800,1024]{2,1,0:T(8,128)(2,1)S(1)}, bf16[2,800,1024]{2,1,0:T(8,128)(2,1)S(1)}, u32[]{:S(2)}, u32[]{:S(2)}) collective-permute-start(bf16[2,800,1024]{2,1,0:T(8,128)(2,1)S(1)} %get-tuple-element.33.refs_0_), channel_id=1, source_target_pairs={{0,1},{1,2},{2,3},{3,0},{4,5},{5,6},{6,7},{7,4},{8,9},{9,10},{10,1... | collective-permute-start | bytes 9830408 | tf_op jit(solution)/shard_map/ppermute | solution.py:214
  704.6 74.0 %collective-permute-start.9 = (bf16[2,800,1024]{2,1,0:T(8,128)(2,1)S(1)}, bf16[2,800,1024]{2,1,0:T(8,128)(2,1)}, u32[]{:S(2)}, u32[]{:S(2)}) collective-permute-start(bf16[2,800,1024]{2,1,0:T(8,128)(2,1)S(1)} %get-tuple-element.33.refs_0_), channel_id=1, source_target_pairs={{0,3},{1,0},{2,1},{3,2},{4,7},{5,4},{6,5},{7,6},{8,11},{9,8},{10,9... | collective-permute-start | bytes 9830408 | tf_op jit(solution)/shard_map/ppermute | solution.py:215
  717.1 131.6 %collective-permute-start.4 = (bf16[2,256,3200]{2,1,0:T(8,128)(2,1)S(1)}, bf16[2,256,3200]{2,1,0:T(8,128)(2,1)S(1)}, u32[]{:S(2)}, u32[]{:S(2)}) collective-permute-start(bf16[2,256,3200]{2,1,0:T(8,128)(2,1)S(1)} %get-tuple-element.36.refs_0_), channel_id=1, source_target_pairs={{0,1},{1,2},{2,3},{3,0},{4,5},{5,6},{6,7},{7,4},{8,9},{9,10},{10,1... | collective-permute-start | bytes 9830408 | tf_op jit(solution)/shard_map/ppermute | solution.py:214
  717.2 132.9 %collective-permute-start.5 = (bf16[2,256,3200]{2,1,0:T(8,128)(2,1)S(1)}, bf16[2,256,3200]{2,1,0:T(8,128)(2,1)}, u32[]{:S(2)}, u32[]{:S(2)}) collective-permute-start(bf16[2,256,3200]{2,1,0:T(8,128)(2,1)S(1)} %get-tuple-element.36.refs_0_), channel_id=1, source_target_pairs={{0,3},{1,0},{2,1},{3,2},{4,7},{5,4},{6,5},{7,6},{8,11},{9,8},{10,9... | collective-permute-start | bytes 9830408 | tf_op jit(solution)/shard_map/ppermute | solution.py:215
  730.7 188.2 %collective-permute-start = (bf16[2,256,3200]{2,1,0:T(8,128)(2,1)S(1)}, bf16[2,256,3200]{2,1,0:T(8,128)(2,1)S(1)}, u32[]{:S(2)}, u32[]{:S(2)}) collective-permute-start(bf16[2,256,3200]{2,1,0:T(8,128)(2,1)S(1)} %get-tuple-element.39.refs_0_), channel_id=1, source_target_pairs={{0,1},{1,2},{2,3},{3,0},{4,5},{5,6},{6,7},{7,4},{8,9},{9,10},{10,1... | collective-permute-start | bytes 9830408 | tf_op jit(solution)/shard_map/ppermute | solution.py:214
  778.5 141.8 %copy-start = (bf16[2,800,1024]{2,1,0:T(8,128)(2,1)}, bf16[2,800,1024]{2,1,0:T(8,128)(2,1)S(1)}, u32[]{:S(2)}) copy-start(bf16[2,800,1024]{2,1,0:T(8,128)(2,1)S(1)} %collective-permute-done.8.refs_1_) | copy-start | bytes 9830404
  778.5 141.8 %collective-permute-start.1 = (bf16[2,256,3200]{2,1,0:T(8,128)(2,1)S(1)}, bf16[2,256,3200]{2,1,0:T(8,128)(2,1)S(1)}, u32[]{:S(2)}, u32[]{:S(2)}) collective-permute-start(bf16[2,256,3200]{2,1,0:T(8,128)(2,1)S(1)} %get-tuple-element.39.refs_0_), channel_id=1, source_target_pairs={{0,3},{1,0},{2,1},{3,2},{4,7},{5,4},{6,5},{7,6},{8,11},{9,8},{10,9... | collective-permute-start | bytes 9830408 | tf_op jit(solution)/shard_map/ppermute | solution.py:215
  778.6 175.4 %collective-permute-start.10 = (bf16[800,1024]{1,0:T(8,128)(2,1)S(1)}, bf16[800,1024]{1,0:T(8,128)(2,1)S(1)}, u32[]{:S(2)}, u32[]{:S(2)}) collective-permute-start(bf16[800,1024]{1,0:T(8,128)(2,1)S(1)} %slice_bitcast_fusion.1), channel_id=1, source_target_pairs={{0,1},{1,2},{2,3},{3,0},{4,5},{5,6},{6,7},{7,4},{8,9},{9,10},{10,1... | collective-permute-start | bytes 4915208 | tf_op jit(solution)/shard_map/ppermute | solution.py:216
  782.3 171.8 %copy-start.15 = (s32[4]{0:T(128)S(1)}, s32[4]{0:T(128)}, u32[]{:S(2)}) copy-start(s32[4]{0:T(128)} %constant.69.clone) | copy-start | bytes 52
  848.7 105.4 %copy-start.2 = (bf16[2,256,3200]{2,1,0:T(8,128)(2,1)}, bf16[2,256,3200]{2,1,0:T(8,128)(2,1)S(1)}, u32[]{:S(2)}) copy-start(bf16[2,256,3200]{2,1,0:T(8,128)(2,1)S(1)} %collective-permute-done.4.refs_1_) | copy-start | bytes 9830404
  848.7 105.4 %collective-permute-start.11 = (bf16[800,1024]{1,0:T(8,128)(2,1)S(1)}, bf16[800,1024]{1,0:T(8,128)(2,1)S(1)}, u32[]{:S(2)}, u32[]{:S(2)}) collective-permute-start(bf16[800,1024]{1,0:T(8,128)(2,1)S(1)} %slice_bitcast_fusion), channel_id=1, source_target_pairs={{0,3},{1,0},{2,1},{3,2},{4,7},{5,4},{6,5},{7,6},{8,11},{9,8},{10,9... | collective-permute-start | bytes 4915208 | tf_op jit(solution)/shard_map/ppermute | solution.py:217
  850.1 139.1 %collective-permute-start.6 = (bf16[256,3200]{1,0:T(8,128)(2,1)}, bf16[256,3200]{1,0:T(8,128)(2,1)}, u32[]{:S(2)}, u32[]{:S(2)}) collective-permute-start(bf16[256,3200]{1,0:T(8,128)(2,1)} %slice_bitcast_fusion.3), channel_id=1, source_target_pairs={{0,1},{1,2},{2,3},{3,0},{4,5},{5,6},{6,7},{7,4},{8,9},{9,10},{10,1... | collective-permute-start | bytes 4915208 | tf_op jit(solution)/shard_map/ppermute | solution.py:216
  918.9 35.1 %copy-start.4 = (bf16[2,256,3200]{2,1,0:T(8,128)(2,1)}, bf16[2,256,3200]{2,1,0:T(8,128)(2,1)S(1)}, u32[]{:S(2)}) copy-start(bf16[2,256,3200]{2,1,0:T(8,128)(2,1)S(1)} %collective-permute-done.refs_1_) | copy-start | bytes 9830404
  918.9 70.2 %collective-permute-start.7 = (bf16[256,3200]{1,0:T(8,128)(2,1)}, bf16[256,3200]{1,0:T(8,128)(2,1)}, u32[]{:S(2)}, u32[]{:S(2)}) collective-permute-start(bf16[256,3200]{1,0:T(8,128)(2,1)} %slice_bitcast_fusion.2), channel_id=1, source_target_pairs={{0,3},{1,0},{2,1},{3,2},{4,7},{5,4},{6,5},{7,6},{8,11},{9,8},{10,9... | collective-permute-start | bytes 4915208 | tf_op jit(solution)/shard_map/ppermute | solution.py:217
  920.3 33.8 %copy-start.6 = (bf16[2,256,3200]{2,1,0:T(8,128)(2,1)}, bf16[2,256,3200]{2,1,0:T(8,128)(2,1)S(1)}, u32[]{:S(2)}) copy-start(bf16[2,256,3200]{2,1,0:T(8,128)(2,1)S(1)} %collective-permute-done.1.refs_2_) | copy-start | bytes 9830404
  920.3 100.7 %collective-permute-start.2 = (bf16[256,3200]{1,0:T(8,128)(2,1)}, bf16[256,3200]{1,0:T(8,128)(2,1)}, u32[]{:S(2)}, u32[]{:S(2)}) collective-permute-start(bf16[256,3200]{1,0:T(8,128)(2,1)} %slice_bitcast_fusion.5), channel_id=1, source_target_pairs={{0,1},{1,2},{2,3},{3,0},{4,5},{5,6},{6,7},{7,4},{8,9},{9,10},{10,1... | collective-permute-start | bytes 4915208 | tf_op jit(solution)/shard_map/ppermute | solution.py:216
  954.0 66.9 %collective-permute-start.3 = (bf16[256,3200]{1,0:T(8,128)(2,1)}, bf16[256,3200]{1,0:T(8,128)(2,1)}, u32[]{:S(2)}, u32[]{:S(2)}) collective-permute-start(bf16[256,3200]{1,0:T(8,128)(2,1)} %slice_bitcast_fusion.4), channel_id=1, source_target_pairs={{0,3},{1,0},{2,1},{3,2},{4,7},{5,4},{6,5},{7,6},{8,11},{9,8},{10,9... | collective-permute-start | bytes 4915208 | tf_op jit(solution)/shard_map/ppermute | solution.py:217
  954.1 1.9 copy-start.1
  956.0 33.1 %copy-start.3 = (bf16[2,256,3200]{2,1,0:T(8,128)(2,1)S(1)}, bf16[2,256,3200]{2,1,0:T(8,128)(2,1)}, u32[]{:S(2)}) copy-start(bf16[2,256,3200]{2,1,0:T(8,128)(2,1)} %copy-done.2) | copy-start | bytes 9830404
  963.9 57.1 %copy-start.5 = (bf16[2,256,3200]{2,1,0:T(8,128)(2,1)S(1)}, bf16[2,256,3200]{2,1,0:T(8,128)(2,1)}, u32[]{:S(2)}) copy-start(bf16[2,256,3200]{2,1,0:T(8,128)(2,1)} %copy-done.4) | copy-start | bytes 9830404
  963.9 57.1 %copy-start.7 = (bf16[2,256,3200]{2,1,0:T(8,128)(2,1)S(1)}, bf16[2,256,3200]{2,1,0:T(8,128)(2,1)}, u32[]{:S(2)}) copy-start(bf16[2,256,3200]{2,1,0:T(8,128)(2,1)} %copy-done.6) | copy-start | bytes 9830404
Sparse Core Ops, SparseCore 0:
  206.9 64.9 reduce-scatter.8
  327.1 117.5 reduce-scatter.4
  447.6 61.7 reduce-scatter.10
  560.2 114.3 reduce-scatter.6

commit v2 on v1

--- a/solution.py
+++ b/solution.py
@@ -68,97 +68,595 @@
         compiler_params=pltpu.CompilerParams(vmem_limit_bytes=60 << 20, dimension_semantics=("arbitrary","arbitrary")),
         cost_estimate=pl.CostEstimate(flops=2*t*d*ff, bytes_accessed=2*(t*ff+t*d+d*ff), transcendentals=0), name="dwd")(actT, dh, after)
 
-def bwd_kernel(J, nt, ff, sub, keep, gate_ref, up_ref, dh_ref, wd_ref, aT_ref, after_ref, dw_ref, *refs):
-    if keep: dgo_ref, duo_ref, dg0, du0, dg1, du1 = refs
-    else: dg0, du0, dg1, du1 = refs
+
+MESH = pl.DeviceIdType.MESH
+
+
+class Ring:
+    def __init__(self, n, jobs, stages, sems, ss_refs):
+        self.n, self.jobs, self.stages, self.ss = n, jobs, stages, ss_refs
+        self.out_send, self.stage_send, self.arrive, self.load = sems
+        self.me = lax.axis_index("dp")
+
+    def enter(self):
+        barrier = pltpu.get_barrier_semaphore()
+        for k in range(1, self.n):
+            pl.semaphore_signal(barrier, inc=1, device_id={"dp": lax.rem(self.me + k, self.n)}, device_id_type=MESH)
+        pl.semaphore_wait(barrier, self.n - 1)
+        for ss in self.ss:
+            ss[...] = jnp.zeros_like(ss)
+
+    def owner(self, h, way):
+        return lax.rem(self.me + (2 * self.n - 1 - h if way == 0 else 1 + h), self.n)
+
+    def send(self, k, h, way):
+        job = self.jobs[k]
+        to = lax.rem(self.me + (1 if way == 0 else self.n - 1), self.n)
+        if h == 0:
+            src, sem = job["piece"](way, self.owner(0, way)), self.out_send.at[k, way]
+        else:
+            src, sem = self.staged(k, h, way)[0], self.stage_send.at[job["kind"], k % 2, h - 1, way]
+        return pltpu.make_async_remote_copy(
+            src_ref=src,
+            dst_ref=job["slot"](h, way),
+            send_sem=sem,
+            recv_sem=self.arrive.at[k, h, way],
+            device_id={"dp": to},
+            device_id_type=MESH,
+        )
+
+    def staged(self, k, h, way):
+        kind, wide = self.jobs[k]["kind"], self.jobs[k]["wide"]
+        return [stage.at[k % 2, h - 1, way, :, pl.ds(0, wide)] for stage in self.stages[kind]]
+
+    def loads(self, k, h, way):
+        job = self.jobs[k]
+        came, mine = self.staged(k, h, way)
+        sem = self.load.at[job["kind"], k % 2]
+        return (
+            pltpu.make_async_copy(job["slot"](h - 1, way), came, sem.at[0, h - 1, way]),
+            pltpu.make_async_copy(job["piece"](way, self.owner(h, way)), mine, sem.at[1, h - 1, way]),
+        )
+
+    def result(self, k, way):
+        job = self.jobs[k]
+        came, _ = self.staged(k, self.n - 1, way)
+        return pltpu.make_async_copy(came, job["out"](way), self.stage_send.at[job["kind"], k % 2, self.n - 2, way])
+
+    def hop_a(self, k, h, before):
+        for way in (0, 1):
+            if before is not None:
+                self.settle(before, h, way)
+            self.send(k, h - 1, way).wait_recv()
+            for copy in self.loads(k, h, way):
+                copy.start()
+
+    def settle(self, k, h, way):
+        if h < self.n - 1:
+            self.send(k, h, way).wait_send()
+        else:
+            self.result(k, way).wait()
+
+    def hop_b(self, k, h):
+        kind = self.jobs[k]["kind"]
+        ss = self.ss[kind]
+        for way in (0, 1):
+            for copy in self.loads(k, h, way):
+                copy.wait()
+            came, mine = self.staged(k, h, way)
+            wide = self.jobs[k]["wide"]
+            rows = 32
+
+            @pl.loop(0, came.shape[0] // rows)
+            def _(r):
+                at = pl.ds(pl.multiple_of(r * rows, rows), rows)
+                total = (came[at, :].astype(F32) + mine[at, :].astype(F32)).astype(BF16)
+                came[at, :] = total
+                if h == self.n - 1:
+                    square = total.astype(F32)
+                    square = square * square
+                    ss[:, :wide] += sum(square[8 * q : 8 * q + 8] for q in range(rows // 8))
+
+            if h < self.n - 1:
+                self.send(k, h, way).start()
+            else:
+                self.result(k, way).start()
+
+    def plan(self, step_us, slack):
+        n, jobs, steps = self.n, self.jobs, len(step_us)
+        todo, came, before, gone = [], {}, {}, {}
+        link = now = 0.0
+        injected, started, left = 0, [], len(jobs) * (n - 1)
+        step = 0
+
+        def put(k, h, at):
+            nonlocal link
+            link = max(link, at) + jobs[k]["us"]
+            gone[k, h] = link + 2.0
+            if h < n - 1:
+                came[k, h + 1] = link + 3.0
+
+        while left:
+            inside = step < steps
+            if not inside and not started:
+                now = max(now, min(came.values(), default=now))
+            for k, h in started:
+                todo.append((step, "b", k, h, None))
+                left -= 1
+                if h < n - 1:
+                    put(k, h, now + 0.7)
+            started = []
+            if injected < len(jobs) and (jobs[injected]["ready"] <= step or not inside) and link <= now + 12:
+                todo.append((step, "inject", injected, 0, None))
+                put(injected, 0, now)
+                injected += 1
+            due = []
+            for (k, h), at in came.items():
+                at = max(at, gone.get((before.get((jobs[k]["kind"], k % 2, h)), h), 0.0))
+                if at + slack * inside <= now or not inside:
+                    due.append((at, (k, h)))
+            due.sort()
+            for _, (k, h) in due[: 2 if inside else 1]:
+                key = jobs[k]["kind"], k % 2, h
+                if any((jobs[i]["kind"], i % 2, g) == key for i, g in started):
+                    continue
+                del came[k, h]
+                todo.append((step, "a", k, h, before.get(key)))
+                before[key] = k
+                started.append((k, h))
+            now += step_us[step] if inside else 2.0 if due else 1.0
+            step += 1
+        self.last = [(k, h) for (_, _, h), k in before.items()]
+        return todo
+
+    def do(self, what, k, h, before):
+        if what == "inject":
+            for way in (0, 1):
+                self.send(k, 0, way).start()
+        elif what == "a":
+            self.hop_a(k, h, before)
+        else:
+            self.hop_b(k, h)
+
+    def follow(self, plan, step, steps):
+        for s in range(steps):
+            if any(at == s for at, *_ in plan):
+
+                @pl.when(step == s)
+                def _():
+                    for at, *what in plan:
+                        if at == s:
+                            self.do(*what)
+
+    def finish(self, plan, steps):
+        for at, *what in plan:
+            if at >= steps:
+                self.do(*what)
+
+    def leave(self):
+        for k, h in self.last:
+            for way in (0, 1):
+                self.settle(k, h, way)
+        for k in range(len(self.jobs)):
+            for way in (0, 1):
+                self.send(k, 0, way).wait_send()
+
+
+def ring_sems(n, jobs):
+    dma = pltpu.SemaphoreType.DMA
+    return [dma((jobs, 2)), dma((2, 2, n - 1, 2)), dma((jobs, n - 1, 2)), dma((2, 2, 2, n - 1, 2))]
+
+
+LINK = 46.6e3
+
+
+def down_jobs(n, count, dwd_ref, slots, out_ref):
+    rows, cols = dwd_ref.shape[0] // n, dwd_ref.shape[1] // 2
+    some = rows // count
+
+    def job(c):
+        def at(way):
+            return pl.ds(way * cols, cols)
+
+        return dict(
+            kind=0,
+            ready=0,
+            us=2 * some * cols / LINK,
+            wide=cols,
+            piece=lambda way, owner: dwd_ref.at[pl.ds(pl.multiple_of(owner * rows + c * some, 16), some), at(way)],
+            slot=lambda h, way: slots.at[c, h, way],
+            out=lambda way: out_ref.at[pl.ds(c * some, some), at(way)],
+        )
+
+    return [job(c) for c in range(count)]
+
+
+def in_jobs(n, spans, dw_ref, slots, out_ref, kind, ready):
+    rows = dw_ref.shape[1] // n
+
+    def job(slot, first, wide):
+        at = pl.ds(first, wide)
+        return dict(
+            kind=kind,
+            ready=ready(first + wide),
+            us=2 * rows * wide / LINK,
+            wide=wide,
+            piece=lambda way, owner: dw_ref.at[way, pl.ds(pl.multiple_of(owner * rows, 16), rows), at],
+            slot=lambda h, way: slots.at[slot, h, way, :, pl.ds(0, wide)],
+            out=lambda way: out_ref.at[way, :, at],
+        )
+
+    return [job(slot, *span) for slot, span in enumerate(spans)]
+
+
+def spans_of(cols, wide, first=0, last=None):
+    return tuple((c, min(wide, cols - c)) for c in range(0, cols, wide))[first:last]
+
+
+DOWN_JOBS = 5
+
+
+def bwd_kernel(cfg, *refs):
+    n, J, nt, ff, sub, keep, spans, slack, last = cfg
+    gate_ref, up_ref, dh_ref, wd_ref, aT_ref, dwd_ref = refs[:6]
+    refs = refs[6:]
+    if last:
+        other_ref, refs = refs[0], refs[1:]
+    dw_ref, slots0, slots1, gd_ref, gg_ref, ss_out = refs[:6]
+    refs = refs[6:]
+    if keep:
+        dgo_ref, duo_ref = refs[:2]
+        refs = refs[2:]
+    dg0, du0, dg1, du1, piece, piece_sem, came0, mine0, came1, mine1, ss0, ss1 = refs[:12]
+    refs = refs[12:]
+    sems, refs = refs[:4], refs[4:]
     j, t = pl.program_id(0), pl.program_id(1)
+    step = j * nt + t
     tt = gate_ref.shape[0]
     nfull, tail = ff // J, ff % J
-    d = aT_ref.shape[0]; q = d // nt
+    d = aT_ref.shape[0]
+    q = d // nt
     rows = pl.ds(pl.multiple_of(t * q, q), q)
+    jobs = down_jobs(n, DOWN_JOBS, dwd_ref, slots0, gd_ref) + in_jobs(
+        n, spans, dw_ref, slots1, gg_ref, 1, lambda cols: (-(-cols // J) + 1) * nt + 2
+    )
+    ring = Ring(n, jobs, ((came0, mine0), (came1, mine1)), sems, (ss0, ss1))
+    steps = (nfull + 2) * nt
+    plan = ring.plan([1.8] * nt + [4.8] * (nt * (nfull - 1)) + [3.4] * nt + [0.9] * nt, slack)
+    @pl.when(step == 0)
+    def _():
+        ring.enter()
+
+    def put_away(parity, way, cols):
+        return pltpu.make_async_copy(piece.at[parity, way, :, pl.ds(0, cols.size)], dw_ref.at[way, rows, cols], piece_sem.at[parity, way])
+
+    parity = lax.rem(t, 2)
+    ring.follow(plan, step, steps)
+
     def stage_a(w, put):
         cols = pl.ds(0, w)
         for r in range(tt // sub):
             rs = pl.ds(r * sub, sub)
             dst = pl.ds(pl.multiple_of(t * tt + r * sub, sub), sub)
             dact = dot_nt(dh_ref[rs, :], wd_ref[cols, :]).astype(BF16).astype(F32)
-            g = gate_ref[rs, cols]; u = up_ref[rs, cols]
-            s = sigmoid(g); silu = g * s
+            g = gate_ref[rs, cols]
+            u = up_ref[rs, cols]
+            s = sigmoid(g)
+            silu = g * s
             dup = (dact * silu).astype(BF16)
             dgate = (dact * u * (s + silu * (1.0 - s))).astype(BF16)
             put(dst, dgate, dup)
-            if keep: dgo_ref[rs, cols] = dgate; duo_ref[rs, cols] = dup
+            if keep:
+                dgo_ref[rs, cols] = dgate
+                duo_ref[rs, cols] = dup
+
     def a_full(dg, du):
-        def put(dst, a, b): dg[dst, :] = a; du[dst, :] = b
+        def put(dst, a, b):
+            dg[dst, :] = a
+            du[dst, :] = b
+
         stage_a(J, put)
+
     def a_tail(dg):
-        def put(dst, a, b): dg[dst, :tail] = a; dg[dst, tail:2*tail] = b
+        def put(dst, a, b):
+            dg[dst, :tail] = a
+            dg[dst, tail : 2 * tail] = b
+
         stage_a(tail, put)
+
     def b_full(dg, du):
-        dw_ref[0] = dot(aT_ref[rows, :], dg[...]).astype(BF16)
-        dw_ref[1] = dot(aT_ref[rows, :], du[...]).astype(BF16)
+        piece[parity, 0] = dot(aT_ref[rows, :], dg[...]).astype(BF16)
+        piece[parity, 1] = dot(aT_ref[rows, :], du[...]).astype(BF16)
+
     def b_tail(dg):
-        o = dot(aT_ref[rows, :], dg[:, :2*tail]).astype(BF16)
-        dw_ref[0, :, :tail] = o[:, :tail]; dw_ref[1, :, :tail] = o[:, tail:]
+        o = dot(aT_ref[rows, :], dg[:, : 2 * tail]).astype(BF16)
+        piece[parity, 0, :, :tail] = o[:, :tail]
+        piece[parity, 1, :, :tail] = o[:, tail:]
+
+    full_cols = pl.ds(pl.multiple_of(jnp.maximum(j - 1, 0) * J, J), J)
+    tail_cols = pl.ds(nfull * J, tail)
+
+    @pl.when((step >= nt + 2) & (step < (nfull + 1) * nt + 2))
+    def _():
+        for way in (0, 1):
+            put_away(parity, way, pl.ds(0, J)).wait()
+
+    @pl.when(step >= (nfull + 1) * nt + 2)
+    def _():
+        for way in (0, 1):
+            put_away(parity, way, tail_cols).wait()
+
     odd = lax.rem(j, 2) == 1
-    assert nfull % 2 == 0
+
     @pl.when(j == 0)
-    def _(): a_full(dg0, du0)
+    def _():
+        a_full(dg0, du0)
+
     @pl.when(odd & (j < nfull))
-    def _(): a_full(dg1, du1); b_full(dg0, du0)
+    def _():
+        a_full(dg1, du1)
+        b_full(dg0, du0)
+
     @pl.when(~odd & (j > 0) & (j < nfull))
-    def _(): a_full(dg0, du0); b_full(dg1, du1)
+    def _():
+        a_full(dg0, du0)
+        b_full(dg1, du1)
+
     @pl.when(j == nfull)
-    def _(): a_tail(dg0); b_full(dg1, du1)
+    def _():
+        a_tail(dg0)
+        b_full(dg1, du1)
+
     @pl.when(j == nfull + 1)
-    def _(): b_tail(dg0)
-
-def bwd(layer, gate, up, dh, wd, aT, after, J=512, tt=1024, sub=512, keep=True):
-    t, ff = gate.shape; d = dh.shape[1]; nt = t // tt; nj = -(-ff // J)
+    def _():
+        b_tail(dg0)
+
+    @pl.when((j > 0) & (j <= nfull))
+    def _():
+        for way in (0, 1):
+            put_away(parity, way, full_cols).start()
+
+    @pl.when(j == nfull + 1)
+    def _():
+        for way in (0, 1):
+            put_away(parity, way, tail_cols).start()
+
+    @pl.when(step == steps - 1)
+    def _():
+        for p in (0, 1):
+            for way in (0, 1):
+                put_away(p, way, tail_cols).wait()
+        ring.finish(plan, steps)
+        total = jnp.sum(ss0[...]) + jnp.sum(ss1[...])
+        if last:
+            all_ss, ss_send, ss_recv = refs
+            total = total + other_ref[0, 0]
+            all_ss[ring.me] = jnp.full(all_ss.shape[1:], total, F32)
+        ring.leave()
+        if last:
+
+            def tell(k):
+                peer = lax.rem(ring.me + k, n)
+                return pltpu.make_async_remote_copy(
+                    src_ref=all_ss.at[ring.me],
+                    dst_ref=all_ss.at[ring.me],
+                    send_sem=ss_send.at[k - 1],
+                    recv_sem=ss_recv.at[k - 1],
+                    device_id={"dp": peer},
+                    device_id_type=MESH,
+                )
+
+            for k in range(1, n):
+                tell(k).start()
+            for k in range(1, n):
+                tell(k).wait()
+            total = jnp.max(sum(all_ss[k] for k in range(n)))
+        ss_out[...] = jnp.full(ss_out.shape, total, F32)
+
+
+def bwd(layer, n, gate, up, dh, wd, aT, dwd, other=None, J=512, tt=1024, sub=256, spans=(), slack=0.0):
+    keep, last = other is None, other is not None
+    t, ff = gate.shape
+    d = dh.shape[1]
+    nt = t // tt
+    nj = -(-ff // J)
     once = pl.Buffered(1)
-    jj = lambda j: jnp.minimum(j, nj - 1)
-    ti = lambda j, i: jnp.where(j == nj, nt - 1, i)
+
+    def jj(j):
+        return jnp.minimum(j, nj - 1)
+
+    def ti(j, i):
+        return jnp.where(j == nj, nt - 1, i)
+
     tile = pl.BlockSpec((tt, J), lambda j, i: (ti(j, i), jj(j)))
-    in_specs = [tile, tile, pl.BlockSpec((tt, d), lambda j, i: (ti(j, i), 0)), pl.BlockSpec((None, J, d), lambda j, i: (layer, jj(j), 0)),
-        pl.BlockSpec((d, t), lambda j, i: (0, 0), pipeline_mode=once), pl.BlockSpec(memory_space=pl.ANY)]
-    out_specs = [pl.BlockSpec((2, d // nt, J), lambda j, i: (0, jnp.where(j == 0, 0, i), jnp.maximum(j - 1, 0)))] + [tile] * (2 * keep)
-    out_shape = [jax.ShapeDtypeStruct((2, d, ff), BF16)] + [jax.ShapeDtypeStruct((t, ff), BF16)] * (2 * keep)
-    return pl.pallas_call(functools.partial(bwd_kernel, J, nt, ff, sub, keep), grid=(nj + 1, nt), in_specs=in_specs,
-        out_specs=out_specs, out_shape=out_shape, scratch_shapes=[pltpu.VMEM((t, J), BF16)] * 4,
-        compiler_params=pltpu.CompilerParams(vmem_limit_bytes=61 << 20, dimension_semantics=("arbitrary", "arbitrary")),
-        cost_estimate=pl.CostEstimate(flops=6*t*d*ff, bytes_accessed=8*t*ff, transcendentals=t*ff), name=f"bwd{layer}")(gate, up, dh, wd, aT, after)
-
-def dx_kernel(n, sub, dg_ref, du_ref, wg_ref, wu_ref, h_ref, dh_ref, o_ref, da_ref):
+    anywhere = pl.BlockSpec(memory_space=pl.ANY)
+    small = pl.BlockSpec((8, 128), lambda j, i: (0, 0))
+    ins = [gate, up, dh, wd, aT, dwd]
+    in_specs = [
+        tile,
+        tile,
+        pl.BlockSpec((tt, d), lambda j, i: (ti(j, i), 0)),
+        pl.BlockSpec((None, J, d), lambda j, i: (layer, jj(j), 0)),
+        pl.BlockSpec((d, t), lambda j, i: (0, 0), pipeline_mode=once),
+        anywhere,
+    ]
+    if last:
+        ins.append(other)
+        in_specs.append(small)
+    wide = max(w for _, w in spans)
+    down_rows, down_wide = ff // n // DOWN_JOBS, d // 2
+    slots = [(DOWN_JOBS, n - 1, 2, down_rows, down_wide), (len(spans), n - 1, 2, d // n, wide)]
+    out_shape = [jax.ShapeDtypeStruct(s, BF16) for s in [(2, d, ff), *slots, (ff // n, d), (2, d // n, ff)]]
+    out_shape.append(jax.ShapeDtypeStruct((8, 128), F32))
+    out_specs = [anywhere] * 5 + [small]
+    if keep:
+        out_shape += [jax.ShapeDtypeStruct((t, ff), BF16)] * 2
+        out_specs += [tile] * 2
+    scratch = [pltpu.VMEM((t, J), BF16)] * 4 + [pltpu.VMEM((2, 2, d // nt, J), BF16), pltpu.SemaphoreType.DMA((2, 2))]
+    scratch += [pltpu.VMEM((2, n - 1, 2, down_rows, down_wide), BF16)] * 2 + [pltpu.VMEM((2, n - 1, 2, d // n, wide), BF16)] * 2
+    scratch += [pltpu.VMEM((8, down_wide), F32), pltpu.VMEM((8, wide), F32)]
+    scratch += ring_sems(n, DOWN_JOBS + len(spans))
+    if last:
+        scratch += [pltpu.VMEM((n, 8, 128), F32), pltpu.SemaphoreType.DMA((n - 1,)), pltpu.SemaphoreType.DMA((n - 1,))]
+    cfg = (n, J, nt, ff, sub, keep, spans, slack, last)
+    return pl.pallas_call(
+        functools.partial(bwd_kernel, cfg),
+        grid=(nj + 1, nt),
+        in_specs=in_specs,
+        out_specs=out_specs,
+        out_shape=out_shape,
+        scratch_shapes=scratch,
+        compiler_params=pltpu.CompilerParams(
+            vmem_limit_bytes=62 << 20, dimension_semantics=("arbitrary", "arbitrary"), collective_id=1 + layer, has_side_effects=True
+        ),
+        cost_estimate=pl.CostEstimate(flops=6 * t * d * ff, bytes_accessed=8 * t * ff, transcendentals=t * ff),
+        name=f"bwd{layer}",
+    )(*ins)
+
+
+def dwd_ring_kernel(n, steps, spans, slack, actT_ref, dh_ref, dw_ref, gg_in, ss_in, o_ref, slots, gg_ref, ss_out, came, mine, ss, *sems):
     i = pl.program_id(0)
-    def epi(rs):
-        da = da_ref[rs, :].astype(BF16).astype(F32)
-        wide = h_ref[rs, :].astype(F32)
+    ring = Ring(n, in_jobs(n, spans, dw_ref, slots, gg_ref, 0, lambda cols: 0), ((came, mine),), sems, (ss,))
+    plan = ring.plan([3.4] * steps, slack)
+
+    @pl.when(i == 0)
+    def _():
+        ring.enter()
+
+    ring.follow(plan, i, steps)
+    o_ref[...] = dot(actT_ref[...], dh_ref[...]).astype(BF16)
+
+    @pl.when(i == steps - 1)
+    def _():
+        ring.finish(plan, steps)
+        ring.leave()
+        ss_out[...] = ss_in[...] + jnp.sum(ss[...])
+
+
+def dwd_ring(n, actT, dh, dw, gg, ss, spans, rb=320, slack=0.0):
+    ff, t = actT.shape
+    d = dh.shape[1]
+    steps = ff // rb
+    wide = max(w for _, w in spans)
+    anywhere = pl.BlockSpec(memory_space=pl.ANY)
+    small = pl.BlockSpec((8, 128), lambda i: (0, 0))
+    return pl.pallas_call(
+        functools.partial(dwd_ring_kernel, n, steps, spans, slack),
+        grid=(steps,),
+        in_specs=[
+            pl.BlockSpec((rb, t), lambda i: (i, 0)),
+            pl.BlockSpec((t, d), lambda i: (0, 0), pipeline_mode=pl.Buffered(1)),
+            anywhere,
+            anywhere,
+            small,
+        ],
+        out_specs=[pl.BlockSpec((rb, d), lambda i: (i, 0)), anywhere, anywhere, small],
+        out_shape=[
+            jax.ShapeDtypeStruct((ff, d), BF16),
+            jax.ShapeDtypeStruct((len(spans), n - 1, 2, d // n, wide), BF16),
+            jax.ShapeDtypeStruct(gg.shape, BF16),
+            jax.ShapeDtypeStruct((8, 128), F32),
+        ],
+        scratch_shapes=[pltpu.VMEM((2, n - 1, 2, d // n, wide), BF16)] * 2 + [pltpu.VMEM((8, wide), F32)] + ring_sems(n, len(spans)),
+        input_output_aliases={3: 2},
+        compiler_params=pltpu.CompilerParams(
+            vmem_limit_bytes=60 << 20, dimension_semantics=("arbitrary",), collective_id=4, has_side_effects=True
+        ),
+        cost_estimate=pl.CostEstimate(flops=2 * t * d * ff, bytes_accessed=2 * (t * ff + t * d + d * ff), transcendentals=0),
+        name="dwd_ring",
+    )(actT, dh, dw, gg, ss)
+
+
+def dx_kernel(cfg, dg_ref, du_ref, wg_ref, wu_ref, h_ref, dh_ref, dw_ref, gg_in, ss_in, o_ref, slots, gg_ref, ss_out, da_ref, came, mine, ss, *sems):
+    n, steps, spans, slack = cfg
+    i = pl.program_id(0)
+    ring = Ring(n, in_jobs(n, spans, dw_ref, slots, gg_ref, 0, lambda cols: 0), ((came, mine),), sems, (ss,))
+    plan = ring.plan([4.2] * steps + [1.0], slack)
+
+    @pl.when(i == 0)
+    def _():
+        ring.enter()
+
+    ring.follow(plan, i, steps + 1)
+
+    def epi():
+        da = da_ref[...].astype(BF16).astype(F32)
+        wide = h_ref[...].astype(F32)
         scale = lax.rsqrt(jnp.mean(wide * wide, -1, keepdims=True) + 1e-6)
         mean = jnp.mean(da * wide, -1, keepdims=True)
         dw = da * scale - wide * (scale * scale * scale * mean)
-        o_ref[rs, :] = dh_ref[rs, :] + dw.astype(BF16)
-    def mm(rs): da_ref[rs, :] = dot_nt(dg_ref[rs, :], wg_ref[...]) + dot_nt(du_ref[rs, :], wu_ref[...])
-    blocks = [pl.ds(r * sub, sub) for r in range(dg_ref.shape[0] // sub)]
+        o_ref[...] = dh_ref[...] + dw.astype(BF16)
+
+    def mm():
+        da_ref[...] = dot_nt(dg_ref[...], wg_ref[...]) + dot_nt(du_ref[...], wu_ref[...])
+
     @pl.when(i == 0)
     def _():
-        for rs in blocks: mm(rs)
-    @pl.when((i > 0) & (i < n))
-    def _():
-        for rs in blocks: epi(rs); mm(rs)
-    @pl.when(i == n)
-    def _():
-        for rs in blocks: epi(rs)
-
-def dx(layer, dg, du, wg, wu, h, dh, tb=512, sub=512):
-    t, ff = dg.shape; d = dh.shape[1]; once = pl.Buffered(1); n = t // tb
-    cur = lambda i: (jnp.minimum(i, n - 1), 0)
-    prv = lambda i: (jnp.maximum(i - 1, 0), 0)
+        mm()
+
+    @pl.when((i > 0) & (i < steps))
+    def _():
+        epi()
+        mm()
+
+    @pl.when(i == steps)
+    def _():
+        epi()
+        ring.finish(plan, steps + 1)
+        ring.leave()
+        ss_out[...] = ss_in[...] + jnp.sum(ss[...])
+
+
+def dx(layer, n, dg, du, wg, wu, h, dh, dw, gg, ss, tb=256, spans=(), slack=0.0):
+    t, ff = dg.shape
+    d = dh.shape[1]
+    once = pl.Buffered(1)
+    steps = t // tb
+
+    def cur(i):
+        return (jnp.minimum(i, steps - 1), 0)
+
+    def prv(i):
+        return (jnp.maximum(i - 1, 0), 0)
+
     w_spec = pl.BlockSpec((None, d, ff), lambda i: (layer, 0, 0), pipeline_mode=once)
-    return pl.pallas_call(functools.partial(dx_kernel, n, sub), grid=(n + 1,),
-        in_specs=[pl.BlockSpec((tb, ff), cur), pl.BlockSpec((tb, ff), cur), w_spec, w_spec, pl.BlockSpec((tb, d), prv), pl.BlockSpec((tb, d), prv)],
-        out_specs=pl.BlockSpec((tb, d), prv), out_shape=jax.ShapeDtypeStruct((t, d), BF16), scratch_shapes=[pltpu.VMEM((tb, d), F32)],
-        compiler_params=pltpu.CompilerParams(vmem_limit_bytes=60 << 20, dimension_semantics=("arbitrary",)),
-        cost_estimate=pl.CostEstimate(flops=4*t*d*ff, bytes_accessed=4*t*ff, transcendentals=0), name=f"dx{layer}")(dg, du, wg, wu, h, dh)
+    anywhere = pl.BlockSpec(memory_space=pl.ANY)
+    small = pl.BlockSpec((8, 128), lambda i: (0, 0))
+    wide = max(w for _, w in spans)
+    cfg = (n, steps, spans, slack)
+    return pl.pallas_call(
+        functools.partial(dx_kernel, cfg),
+        grid=(steps + 1,),
+        in_specs=[
+            pl.BlockSpec((tb, ff), cur),
+            pl.BlockSpec((tb, ff), cur),
+            w_spec,
+            w_spec,
+            pl.BlockSpec((tb, d), prv),
+            pl.BlockSpec((tb, d), prv),
+            anywhere,
+            anywhere,
+            small,
+        ],
+        out_specs=[pl.BlockSpec((tb, d), prv), anywhere, anywhere, small],
+        out_shape=[
+            jax.ShapeDtypeStruct((t, d), BF16),
+            jax.ShapeDtypeStruct((len(spans), n - 1, 2, d // n, wide), BF16),
+            jax.ShapeDtypeStruct(gg.shape, BF16),
+            jax.ShapeDtypeStruct((8, 128), F32),
+        ],
+        scratch_shapes=[pltpu.VMEM((tb, d), F32)]
+        + [pltpu.VMEM((2, n - 1, 2, d // n, wide), BF16)] * 2
+        + [pltpu.VMEM((8, wide), F32)]
+        + ring_sems(n, len(spans)),
+        input_output_aliases={7: 2},
+        compiler_params=pltpu.CompilerParams(
+            vmem_limit_bytes=60 << 20, dimension_semantics=("arbitrary",), collective_id=3, has_side_effects=True
+        ),
+        cost_estimate=pl.CostEstimate(flops=4 * t * d * ff, bytes_accessed=4 * t * ff, transcendentals=0),
+        name=f"dx{layer}",
+    )(dg, du, wg, wu, h, dh, dw, gg, ss)
+
 
 def place_kernel(own_ref, left_ref, right_ref, far0_ref, far1_ref, out_ref, send):
     k = pl.program_id(0)
@@ -234,22 +732,15 @@
         a0, g0, u0, act0, h1 = fwd(0, x, wg, wu, wd)
         a1, g1, u1, act1 = fwd(1, h1, wg, wu)
 
-        def scattered(t):
-            return lax.psum_scatter(t, "dp", scatter_dimension=t.ndim - 2, tiled=True)
-
+        ff = wg.shape[2]
         mine = dwd(act1, dy, act1, rb=800)
-        dwd1 = scattered(mine)
-        dgu1, dg, du = bwd(1, g1, u1, dy, wd, a1, mine, sub=256, keep=True)
-        dgu1 = scattered(dgu1)
-        dh = dx(1, dg, du, wg, wu, h1, dy)
-        mine = dwd(act0, dh, dwd1, rb=800)
-        dwd0 = scattered(mine)
-        dgu0, = bwd(0, g0, u0, dh, wd, a0, dgu1, sub=256, keep=False)
-        dgu0 = scattered(dgu0)
-        grads = [jnp.stack(p).astype(F32) for p in ((dgu0[0], dgu1[0]), (dgu0[1], dgu1[1]), (dwd0, dwd1))]
-        total = lax.psum(sum(jnp.sum(g * g) for g in grads), "dp")
+        dw1, _, _, gd1, gg1, ss, dg, du = bwd(1, n, g1, u1, dy, wd, a1, mine, spans=spans_of(ff, 512, 0, 2), slack=2.0)
+        dh, _, gg1, ss = dx(1, n, dg, du, wg, wu, h1, dy, dw1, gg1, ss, spans=spans_of(ff, 512, 2, 5), slack=1.0)
+        mine, _, gg1, ss = dwd_ring(n, act0, dh, dw1, gg1, ss, spans_of(ff, 512, 5))
+        _, _, _, gd0, gg0, ss = bwd(0, n, g0, u0, dh, wd, a0, mine, ss, spans=spans_of(ff, 256))
+        grads = [jnp.stack(p).astype(F32) for p in ((gg0[0], gg1[0]), (gg0[1], gg1[1]), (gd0, gd1))]
         count = sum(w.size for w in (wg, wu, wd))
-        factor = jnp.minimum(1.0, 0.5 * lax.rsqrt(total / count + 1e-30))
+        factor = jnp.minimum(1.0, 0.5 * lax.rsqrt(ss[0, 0] / count + 1e-30))
         me = lax.axis_index("dp")
         new = []
         for w, mm, vv, g in zip((wg, wu, wd), m, v, grads):

time: 1040 us -> 990 us (0.952)
  waiting for transfers between devices: 376 us -> 248 us
  Pallas kernels: 563 us -> 667 us
  between operations: 17 us -> 1.86 us
    pallas_call x3 -> x4, Pallas kernels: 306 us -> 443 us  [the longest x2 322 us: bwd(): pl.pallas_call(functools.partial(bwd_kernel, cfg), grid=(nj + 1, nt), in_...]
    reduce_scatter x4 -> x0, waiting for transfers between devices: 119 us -> none  [scattered(): return lax.psum_scatter(t, 'dp', scatter_dimension=t.ndim - 2, tiled=True)]
    pallas_call x2 -> x1, Pallas kernels: 68.2 us -> 34.1 us  [dwd(): pl.pallas_call(dwd_kernel, grid=(d // cb, ff // rb), in_specs=[pl.BlockSp...]
  transfers between devices with their start and end apart: 16 -> 12, of which waited for: 8 -> 6; matrix products, arithmetic and copies ran while one was open for 4% -> 4% of each run, Pallas kernels for 34% -> 2%
where the time goes in v2:
time: 990 us; the launch traced here: 981 us
  Pallas kernels  667 us (67%)
  waiting for transfers between devices  248 us (25%)
  other arithmetic  33.5 us (3%)
  local copies, waits for them, and re-layouts  18 us (2%)
  starting transfers between devices  12.4 us (1%)
    pallas_call x2, Pallas kernels, bwd(): pl.pallas_call(functools.partial(bwd_kernel, cfg), grid=(nj + 1, nt), in_...  322 us
    ppermute x3, waiting for transfers between devices, gathered(): left = lax.ppermute(own, 'dp', to_right)  171 us
    pallas_call x2, Pallas kernels, fwd(): pl.pallas_call(functools.partial(fwd_kernel, chunk, wd is not None), grid...  165 us
    pallas_call x1, Pallas kernels, dx(): pl.pallas_call(functools.partial(dx_kernel, cfg), grid=(steps + 1,), in_s...  78.5 us
    ppermute x3, waiting for transfers between devices, gathered(): far0 = lax.ppermute(left[0], 'dp', to_right)  76.1 us
    pallas_call x1, Pallas kernels, dwd_ring(): pl.pallas_call(functools.partial(dwd_ring_kernel, n, steps, spans, slack)...  43.3 us
    pallas_call x1, Pallas kernels, dwd(): pl.pallas_call(dwd_kernel, grid=(d // cb, ff // rb), in_specs=[pl.BlockSp...  34.1 us
    convert_element_type x3, other arithmetic, adamw(): return ((w - 0.02 * step).astype(BF16), m, v)  33.5 us
  transfers between devices with their start and end apart: 12, of which 6 were waited for; matrix products, arithmetic and copies ran while one was open for 4% of the time, Pallas kernels for 2%

profile of v2, /device:TPU:112, one launch (start us, length us, event | category | flops | bytes accessed | tf_op | source)
XLA Modules:
  0.0 980.5 jit_solution(15284369672881437790)
XLA Ops:
  0.6 96.7 %fwd0.1 = (bf16[1024,4096]{1,0:T(8,128)(2,1)}, f32[4096,3200]{1,0:T(8,128)}, f32[4096,3200]{1,0:T(8,128)}, bf16[3200,4096]{1,0:T(8,128)(2,1)}, bf16[4096,1024]{1,0:T(8,128)(2,1)}) custom-call(bf16[4096,1024]{1,0:T(8,128)(2,1)} %bitcast.19, bf16[2,1024,3200]{2,1,0:T(8,128)(2,1)} %wg_ref.5, bf16[2,1024,3200]{2,1,0:T(8,128)(2,1)} %wu_ref.5, ...), custom_call_target="tpu_custom_call" | custom-call | flops 80530636800 | bytes 175898624 | tf_op jit(solution)/shard_map/fwd0/pallas_call | solution.py:54
  97.4 68.8 %fwd1.1 = (bf16[1024,4096]{1,0:T(8,128)(2,1)}, f32[4096,3200]{1,0:T(8,128)}, f32[4096,3200]{1,0:T(8,128)}, bf16[3200,4096]{1,0:T(8,128)(2,1)}) custom-call(bf16[4096,1024]{1,0:T(8,128)(2,1)} %get-tuple-element.35.h_ref, bf16[2,1024,3200]{2,1,0:T(8,128)(2,1)} %wg_ref.5, bf16[2,1024,3200]{2,1,0:T(8,128)(2,1)} %wu_ref.5), custom_call_target="tpu_custom_call" | custom-call | flops 53687091200 | bytes 169345024 | tf_op jit(solution)/shard_map/fwd1/pallas_call | solution.py:54
  166.1 34.1 %dwd.1.refs_5_ = bf16[3200,1024]{1,0:T(8,128)(2,1)} custom-call(bf16[3200,4096]{1,0:T(8,128)(2,1)} %get-tuple-element.39.actT_ref.after_ref, bf16[4096,1024]{1,0:T(8,128)(2,1)} %bitcast.20, bf16[3200,4096]{1,0:T(8,128)(2,1)} %get-tuple-element.39.actT_ref.after_ref), custom_call_target="tpu_custom_call" | custom-call | flops 26843545600 | bytes 41156608 | tf_op jit(solution)/shard_map/dwd/pallas_call | solution.py:65
  200.2 137.5 %bwd1.1 = (bf16[2,1024,3200]{2,1,0:T(8,128)(2,1)}, bf16[5,3,2,160,512]{4,3,2,1,0:T(8,128)(2,1)}, bf16[2,3,2,256,512]{4,3,2,1,0:T(8,128)(2,1)}, bf16[800,1024]{1,...) custom-call(f32[4096,3200]{1,0:T(8,128)} %get-tuple-element.36.refs_, ...), custom_call_target="tpu_custom_call" | custom-call | flops 80530636800 | bytes 104857600 | tf_op jit(solution)/shard_map/bwd1/pallas_call | solution.py:502
  337.7 78.5 %dx1.1 = (bf16[4096,1024]{1,0:T(8,128)(2,1)}, bf16[3,3,2,256,512]{4,3,2,1,0:T(8,128)(2,1)}, bf16[2,256,3200]{2,1,0:T(8,128)(2,1)}, f32[8,128]{1,0:T(8,128)}) custom-call(bf16[4096,3200]{1,0:T(8,128)(2,1)} %get-tuple-element.40.dg_ref, bf16[4096,3200]{1,0:T(8,128)(2,1)} %get-tuple-element.41.du_ref, ...), custom_call_target="tpu_custom_call", output_to_operand_aliasing={{2}: (7, {})} | custom-call | flops 53687091200 | bytes 52428800 | tf_op jit(solution)/shard_map/dx1/pallas_call | solution.py:627
  416.2 43.3 %dwd_ring.1 = (bf16[3200,1024]{1,0:T(8,128)(2,1)}, bf16[2,3,2,256,512]{4,3,2,1,0:T(8,128)(2,1)}, bf16[2,256,3200]{2,1,0:T(8,128)(2,1)}, f32[8,128]{1,0:T(8,128)}) custom-call(bf16[3200,4096]{1,0:T(8,128)(2,1)} %get-tuple-element.47.actT_ref, bf16[4096,1024]{1,0:T(8,128)(2,1)} %get-tuple-element.45.dh_ref.refs_2_, ...), custom_call_target="tpu_custom_call", output_to_operand_aliasing={{2}: (3, {})} | custom-call | flops 26843545600 | bytes 41156608 | tf_op jit(solution)/shard_map/dwd_ring/pallas_call | solution.py:543
  459.5 184.2 %bwd0.1 = (bf16[2,1024,3200]{2,1,0:T(8,128)(2,1)}, bf16[5,3,2,160,512]{4,3,2,1,0:T(8,128)(2,1)}, bf16[13,3,2,256,256]{4,3,2,1,0:T(8,128)(2,1)}, bf16[800,1024]{1...) custom-call(f32[4096,3200]{1,0:T(8,128)} %get-tuple-element.33.refs_0_, ...), custom_call_target="tpu_custom_call" | custom-call | flops 80530636800 | bytes 104857600 | tf_op jit(solution)/shard_map/bwd0/pallas_call | solution.py:502
  643.6 1.2 slice.35
  645.5 11.7 %fusion.8 = (bf16[2,800,1024]{2,1,0:T(8,128)(2,1)S(1)}, f32[2,800,1024]{2,1,0:T(8,128)}, f32[2,800,1024]{2,1,0:T(8,128)}) fusion(bf16[2,3200,1024]{2,1,0:T(8,128)(2,1)} %refs_3_.3, s32[]{:T(128)S(6)} %select_n.26, f32[]{:T(128)} %bitcast.2, bf16[1,800,1024]{2,1,0:T(8,128)(2,1)} %bitcast.17, bf16[1,800,1024]{2,1,0:T(8,128)(2,1)} %bitcast.18, ...), kind=kLoop, calls=%fused_computation.17 | loop fusion | flops 32768000 | bytes 36044808 | tf_op jit(solution)/shard_map/convert_element_type | solution.py:723
  657.2 0.7 collective-permute-start.8
  658.0 2.5 collective-permute-start.9
  660.5 5.8 fusion.16
  666.3 0.0 copy-start.8
  666.3 0.0 copy-start.9
  666.3 11.4 %fusion.5 = (bf16[2,256,3200]{2,1,0:T(8,128)(2,1)S(1)}, f32[2,256,3200]{2,1,0:T(8,128)}, f32[2,256,3200]{2,1,0:T(8,128)}) fusion(bf16[2,1024,3200]{2,1,0:T(8,128)(2,1)} %wu_ref.5, s32[]{:T(128)S(6)} %select_n.23, f32[]{:T(128)} %bitcast.2, bf16[1,256,3200]{2,1,0:T(8,128)(2,1)} %get-tuple-element.71, bf16[1,256,3200]{2,1,0:T(8,128)(2,1)} %get-tuple-element.66, ...), kind=kLoop, calls=%fused_computation.14 | loop fusion | flops 32768000 | bytes 36044808 | tf_op jit(solution)/shard_map/convert_element_type | solution.py:723
  677.7 0.0 collective-permute-start.4
  677.7 3.2 collective-permute-start.5
  680.9 0.0 copy-done.8
  680.9 0.0 copy-done.9
  680.9 10.4 %fusion.2 = (bf16[2,256,3200]{2,1,0:T(8,128)(2,1)S(1)}, f32[2,256,3200]{2,1,0:T(8,128)}, f32[2,256,3200]{2,1,0:T(8,128)}) fusion(bf16[2,1024,3200]{2,1,0:T(8,128)(2,1)} %wg_ref.5, s32[]{:T(128)S(6)} %select_n.23, f32[]{:T(128)} %bitcast.2, bf16[1,256,3200]{2,1,0:T(8,128)(2,1)S(1)} %copy-done.9, bf16[1,256,3200]{2,1,0:T(8,128)(2,1)S(1)} %copy-done.8, ...), kind=kLoop, calls=%fused_computation.11 | loop fusion | flops 32768000 | bytes 36044808 | tf_op jit(solution)/shard_map/convert_element_type | solution.py:723
  691.4 0.0 collective-permute-start
  691.4 40.9 %collective-permute-done.8.refs_1_ = bf16[2,800,1024]{2,1,0:T(8,128)(2,1)} collective-permute-done((bf16[2,800,1024]{2,1,0:T(8,128)(2,1)S(1)}, bf16[2,800,1024]{2,1,0:T(8,128)(2,1)}, u32[]{:S(2)}, u32[]{:S(2)}) %collective-permute-start.8) | collective-permute-done | bytes 3276832 | tf_op jit(solution)/shard_map/ppermute | solution.py:712
  732.2 0.4 collective-permute-start.1
  732.6 1.6 slice_bitcast_fusion.1
  734.2 0.0 collective-permute-done.9.refs_2_
  734.2 1.7 collective-permute-start.10
  735.9 1.6 slice_bitcast_fusion
  737.5 0.0 copy-start.10
  737.5 65.0 %collective-permute-done.4.refs_1_ = bf16[2,256,3200]{2,1,0:T(8,128)(2,1)S(1)} collective-permute-done((bf16[2,256,3200]{2,1,0:T(8,128)(2,1)S(1)}, bf16[2,256,3200]{2,1,0:T(8,128)(2,1)S(1)}, u32[]{:S(2)}, u32[]{:S(2)}) %collective-permute-start.4) | collective-permute-done | bytes 3276832 | tf_op jit(solution)/shard_map/ppermute | solution.py:712
  802.5 0.0 copy-start
  802.5 0.4 collective-permute-start.11
  802.8 1.6 slice_bitcast_fusion.3
  804.5 0.0 collective-permute-done.5.refs_2_
  804.5 0.0 copy-start.2
  804.5 1.3 collective-permute-start.6
  805.8 1.4 slice_bitcast_fusion.2
  807.2 65.5 %collective-permute-done.refs_1_ = bf16[2,256,3200]{2,1,0:T(8,128)(2,1)S(1)} collective-permute-done((bf16[2,256,3200]{2,1,0:T(8,128)(2,1)S(1)}, bf16[2,256,3200]{2,1,0:T(8,128)(2,1)S(1)}, u32[]{:S(2)}, u32[]{:S(2)}) %collective-permute-start) | collective-permute-done | bytes 3276832 | tf_op jit(solution)/shard_map/ppermute | solution.py:712
  872.7 0.0 copy-start.4
  872.7 0.4 collective-permute-start.7
  873.1 1.6 slice_bitcast_fusion.5
  874.7 0.0 collective-permute-done.1.refs_2_
  874.7 0.0 copy-start.6
  874.7 1.3 collective-permute-start.2
  876.0 1.3 slice_bitcast_fusion.4
  877.3 30.5 %collective-permute-done.10.refs_3_ = bf16[800,1024]{1,0:T(8,128)(2,1)S(1)} collective-permute-done((bf16[800,1024]{1,0:T(8,128)(2,1)S(1)}, bf16[800,1024]{1,0:T(8,128)(2,1)S(1)}, u32[]{:S(2)}, u32[]{:S(2)}) %collective-permute-start.10) | collective-permute-done | bytes 1638432 | tf_op jit(solution)/shard_map/ppermute | solution.py:714
  907.8 0.4 collective-permute-start.3
  908.2 0.0 copy-done.10
  908.2 0.0 copy-done
  908.2 0.0 copy-done.2
  908.2 0.0 copy-done.4
  908.2 0.0 copy-done.6
  908.2 0.0 collective-permute-done.11.refs_4_
  908.2 0.0 copy-start.1
  908.2 8.8 place.5
  917.1 25.8 %collective-permute-done.6.refs_3_ = bf16[256,3200]{1,0:T(8,128)(2,1)} collective-permute-done((bf16[256,3200]{1,0:T(8,128)(2,1)}, bf16[256,3200]{1,0:T(8,128)(2,1)}, u32[]{:S(2)}, u32[]{:S(2)}) %collective-permute-start.6) | collective-permute-done | bytes 1638432 | tf_op jit(solution)/shard_map/ppermute | solution.py:714
  942.9 0.0 collective-permute-done.7.refs_4_
  942.9 0.0 copy-done.1
  942.9 1.9 copy-done.3
  944.8 7.9 place.4
  952.7 19.8 %collective-permute-done.2.refs_3_ = bf16[256,3200]{1,0:T(8,128)(2,1)} collective-permute-done((bf16[256,3200]{1,0:T(8,128)(2,1)}, bf16[256,3200]{1,0:T(8,128)(2,1)}, u32[]{:S(2)}, u32[]{:S(2)}) %collective-permute-start.2) | collective-permute-done | bytes 1638432 | tf_op jit(solution)/shard_map/ppermute | solution.py:714
  972.5 0.0 collective-permute-done.3.refs_4_
  972.5 0.0 copy-done.5
  972.5 0.0 copy-done.7
  972.5 7.6 place.3
  (4 shorter events, 0.0 us)
Async XLA Ops:
  657.2 75.0 %collective-permute-start.8 = (bf16[2,800,1024]{2,1,0:T(8,128)(2,1)S(1)}, bf16[2,800,1024]{2,1,0:T(8,128)(2,1)}, u32[]{:S(2)}, u32[]{:S(2)}) collective-permute-start(bf16[2,800,1024]{2,1,0:T(8,128)(2,1)S(1)} %get-tuple-element.57.refs_0_), channel_id=1, source_target_pairs={{0,1},{1,2},{2,3},{3,0},{4,5},{5,6},{6,7},{7,4},{8,9},{9,10},{10,1... | collective-permute-start | bytes 9830408 | tf_op jit(solution)/shard_map/ppermute | solution.py:712
  658.0 76.2 %collective-permute-start.9 = (bf16[2,800,1024]{2,1,0:T(8,128)(2,1)S(1)}, bf16[2,800,1024]{2,1,0:T(8,128)(2,1)}, u32[]{:S(2)}, u32[]{:S(2)}) collective-permute-start(bf16[2,800,1024]{2,1,0:T(8,128)(2,1)S(1)} %get-tuple-element.57.refs_0_), channel_id=1, source_target_pairs={{0,3},{1,0},{2,1},{3,2},{4,7},{5,4},{6,5},{7,6},{8,11},{9,8},{10,9... | collective-permute-start | bytes 9830408 | tf_op jit(solution)/shard_map/ppermute | solution.py:713
  666.3 14.6 %copy-start.8 = (bf16[1,256,3200]{2,1,0:T(8,128)(2,1)S(1)}, bf16[1,256,3200]{2,1,0:T(8,128)(2,1)}, u32[]{:S(2)}) copy-start(bf16[1,256,3200]{2,1,0:T(8,128)(2,1)} %get-tuple-element.67) | copy-start | bytes 4915204
  666.3 14.6 %copy-start.9 = (bf16[1,256,3200]{2,1,0:T(8,128)(2,1)S(1)}, bf16[1,256,3200]{2,1,0:T(8,128)(2,1)}, u32[]{:S(2)}) copy-start(bf16[1,256,3200]{2,1,0:T(8,128)(2,1)} %get-tuple-element.70) | copy-start | bytes 4915204
  677.7 124.8 %collective-permute-start.4 = (bf16[2,256,3200]{2,1,0:T(8,128)(2,1)S(1)}, bf16[2,256,3200]{2,1,0:T(8,128)(2,1)S(1)}, u32[]{:S(2)}, u32[]{:S(2)}) collective-permute-start(bf16[2,256,3200]{2,1,0:T(8,128)(2,1)S(1)} %get-tuple-element.60.refs_0_), channel_id=1, source_target_pairs={{0,1},{1,2},{2,3},{3,0},{4,5},{5,6},{6,7},{7,4},{8,9},{9,10},{10,1... | collective-permute-start | bytes 9830408 | tf_op jit(solution)/shard_map/ppermute | solution.py:712
  677.7 126.8 %collective-permute-start.5 = (bf16[2,256,3200]{2,1,0:T(8,128)(2,1)S(1)}, bf16[2,256,3200]{2,1,0:T(8,128)(2,1)S(1)}, u32[]{:S(2)}, u32[]{:S(2)}) collective-permute-start(bf16[2,256,3200]{2,1,0:T(8,128)(2,1)S(1)} %get-tuple-element.60.refs_0_), channel_id=1, source_target_pairs={{0,3},{1,0},{2,1},{3,2},{4,7},{5,4},{6,5},{7,6},{8,11},{9,8},{10,9... | collective-permute-start | bytes 9830408 | tf_op jit(solution)/shard_map/ppermute | solution.py:713
  691.4 181.3 %collective-permute-start = (bf16[2,256,3200]{2,1,0:T(8,128)(2,1)S(1)}, bf16[2,256,3200]{2,1,0:T(8,128)(2,1)S(1)}, u32[]{:S(2)}, u32[]{:S(2)}) collective-permute-start(bf16[2,256,3200]{2,1,0:T(8,128)(2,1)S(1)} %get-tuple-element.63.refs_0_), channel_id=1, source_target_pairs={{0,1},{1,2},{2,3},{3,0},{4,5},{5,6},{6,7},{7,4},{8,9},{9,10},{10,1... | collective-permute-start | bytes 9830408 | tf_op jit(solution)/shard_map/ppermute | solution.py:712
  732.2 142.4 %collective-permute-start.1 = (bf16[2,256,3200]{2,1,0:T(8,128)(2,1)S(1)}, bf16[2,256,3200]{2,1,0:T(8,128)(2,1)S(1)}, u32[]{:S(2)}, u32[]{:S(2)}) collective-permute-start(bf16[2,256,3200]{2,1,0:T(8,128)(2,1)S(1)} %get-tuple-element.63.refs_0_), channel_id=1, source_target_pairs={{0,3},{1,0},{2,1},{3,2},{4,7},{5,4},{6,5},{7,6},{8,11},{9,8},{10,9... | collective-permute-start | bytes 9830408 | tf_op jit(solution)/shard_map/ppermute | solution.py:713
  734.2 173.6 %collective-permute-start.10 = (bf16[800,1024]{1,0:T(8,128)(2,1)S(1)}, bf16[800,1024]{1,0:T(8,128)(2,1)S(1)}, u32[]{:S(2)}, u32[]{:S(2)}) collective-permute-start(bf16[800,1024]{1,0:T(8,128)(2,1)S(1)} %slice_bitcast_fusion.1), channel_id=1, source_target_pairs={{0,1},{1,2},{2,3},{3,0},{4,5},{5,6},{6,7},{7,4},{8,9},{9,10},{10,1... | collective-permute-start | bytes 4915208 | tf_op jit(solution)/shard_map/ppermute | solution.py:714
  737.5 170.7 %copy-start.10 = (s32[4]{0:T(128)S(1)}, s32[4]{0:T(128)}, u32[]{:S(2)}) copy-start(s32[4]{0:T(128)} %constant.70.clone) | copy-start | bytes 52
  802.5 105.7 %copy-start = (bf16[2,256,3200]{2,1,0:T(8,128)(2,1)}, bf16[2,256,3200]{2,1,0:T(8,128)(2,1)S(1)}, u32[]{:S(2)}) copy-start(bf16[2,256,3200]{2,1,0:T(8,128)(2,1)S(1)} %collective-permute-done.4.refs_1_) | copy-start | bytes 9830404
  802.5 105.8 %collective-permute-start.11 = (bf16[800,1024]{1,0:T(8,128)(2,1)S(1)}, bf16[800,1024]{1,0:T(8,128)(2,1)S(1)}, u32[]{:S(2)}, u32[]{:S(2)}) collective-permute-start(bf16[800,1024]{1,0:T(8,128)(2,1)S(1)} %slice_bitcast_fusion), channel_id=1, source_target_pairs={{0,3},{1,0},{2,1},{3,2},{4,7},{5,4},{6,5},{7,6},{8,11},{9,8},{10,9... | collective-permute-start | bytes 4915208 | tf_op jit(solution)/shard_map/ppermute | solution.py:715
  804.5 103.7 %copy-start.2 = (bf16[2,256,3200]{2,1,0:T(8,128)(2,1)}, bf16[2,256,3200]{2,1,0:T(8,128)(2,1)S(1)}, u32[]{:S(2)}) copy-start(bf16[2,256,3200]{2,1,0:T(8,128)(2,1)S(1)} %collective-permute-done.5.refs_2_) | copy-start | bytes 9830404
  804.5 138.4 %collective-permute-start.6 = (bf16[256,3200]{1,0:T(8,128)(2,1)}, bf16[256,3200]{1,0:T(8,128)(2,1)}, u32[]{:S(2)}, u32[]{:S(2)}) collective-permute-start(bf16[256,3200]{1,0:T(8,128)(2,1)} %slice_bitcast_fusion.3), channel_id=1, source_target_pairs={{0,1},{1,2},{2,3},{3,0},{4,5},{5,6},{6,7},{7,4},{8,9},{9,10},{10,1... | collective-permute-start | bytes 4915208 | tf_op jit(solution)/shard_map/ppermute | solution.py:714
  872.7 35.5 %copy-start.4 = (bf16[2,256,3200]{2,1,0:T(8,128)(2,1)}, bf16[2,256,3200]{2,1,0:T(8,128)(2,1)S(1)}, u32[]{:S(2)}) copy-start(bf16[2,256,3200]{2,1,0:T(8,128)(2,1)S(1)} %collective-permute-done.refs_1_) | copy-start | bytes 9830404
  872.7 70.2 %collective-permute-start.7 = (bf16[256,3200]{1,0:T(8,128)(2,1)}, bf16[256,3200]{1,0:T(8,128)(2,1)}, u32[]{:S(2)}, u32[]{:S(2)}) collective-permute-start(bf16[256,3200]{1,0:T(8,128)(2,1)} %slice_bitcast_fusion.2), channel_id=1, source_target_pairs={{0,3},{1,0},{2,1},{3,2},{4,7},{5,4},{6,5},{7,6},{8,11},{9,8},{10,9... | collective-permute-start | bytes 4915208 | tf_op jit(solution)/shard_map/ppermute | solution.py:715
  874.7 33.5 %copy-start.6 = (bf16[2,256,3200]{2,1,0:T(8,128)(2,1)}, bf16[2,256,3200]{2,1,0:T(8,128)(2,1)S(1)}, u32[]{:S(2)}) copy-start(bf16[2,256,3200]{2,1,0:T(8,128)(2,1)S(1)} %collective-permute-done.1.refs_2_) | copy-start | bytes 9830404
  874.7 97.8 %collective-permute-start.2 = (bf16[256,3200]{1,0:T(8,128)(2,1)}, bf16[256,3200]{1,0:T(8,128)(2,1)}, u32[]{:S(2)}, u32[]{:S(2)}) collective-permute-start(bf16[256,3200]{1,0:T(8,128)(2,1)} %slice_bitcast_fusion.5), channel_id=1, source_target_pairs={{0,1},{1,2},{2,3},{3,0},{4,5},{5,6},{6,7},{7,4},{8,9},{9,10},{10,1... | collective-permute-start | bytes 4915208 | tf_op jit(solution)/shard_map/ppermute | solution.py:714
  907.8 64.7 %collective-permute-start.3 = (bf16[256,3200]{1,0:T(8,128)(2,1)}, bf16[256,3200]{1,0:T(8,128)(2,1)}, u32[]{:S(2)}, u32[]{:S(2)}) collective-permute-start(bf16[256,3200]{1,0:T(8,128)(2,1)} %slice_bitcast_fusion.4), channel_id=1, source_target_pairs={{0,3},{1,0},{2,1},{3,2},{4,7},{5,4},{6,5},{7,6},{8,11},{9,8},{10,9... | collective-permute-start | bytes 4915208 | tf_op jit(solution)/shard_map/ppermute | solution.py:715
  908.2 34.7 %copy-start.1 = (bf16[2,256,3200]{2,1,0:T(8,128)(2,1)S(1)}, bf16[2,256,3200]{2,1,0:T(8,128)(2,1)}, u32[]{:S(2)}) copy-start(bf16[2,256,3200]{2,1,0:T(8,128)(2,1)} %copy-done) | copy-start | bytes 9830404
  942.9 1.9 copy-start.3
  944.8 27.7 %copy-start.5 = (bf16[2,256,3200]{2,1,0:T(8,128)(2,1)S(1)}, bf16[2,256,3200]{2,1,0:T(8,128)(2,1)}, u32[]{:S(2)}) copy-start(bf16[2,256,3200]{2,1,0:T(8,128)(2,1)} %copy-done.4) | copy-start | bytes 9830404
  944.8 27.7 %copy-start.7 = (bf16[2,256,3200]{2,1,0:T(8,128)(2,1)S(1)}, bf16[2,256,3200]{2,1,0:T(8,128)(2,1)}, u32[]{:S(2)}) copy-start(bf16[2,256,3200]{2,1,0:T(8,128)(2,1)} %copy-done.6) | copy-start | bytes 9830404
